TPU v7x, 512 devices: a 8x2x16 block of a 8x8x16 slice. The times are simulated.
512 devices in a mesh: groups: 2 (over y), seq: 16 (over z), fsdp: 8 (over x), sub: 2 (over core).
Axes of the slice: x: 8, y: 2, z: 16, core: 2. Of those that a mesh axis runs over, the one named last changes fastest.
The devices are a block of a 8x8x16 slice.
Arguments:
- tokens: bfloat16 [8192, 8192], P(('groups', 'seq')), parts along dimension 0, may hold values from -400 to 400
- norm_gain: float32 [8192], replicated, may hold values from 0.1 to 1.9
- w_query: bfloat16 [32, 16, 8192], P(('seq', 'sub'), 'fsdp'), may hold values from -0.0625 to 0.0625
- w_key: bfloat16 [32, 16, 8192], P(('seq', 'sub'), 'fsdp'), may hold values from -0.0625 to 0.0625
- w_value: bfloat16 [32, 128, 8192], P(('seq', 'sub'), 'fsdp'), may hold values from -5 to 5
- head_gain: float32 [128], replicated, may hold values from 0.1 to 1.9
- w_out: bfloat16 [32, 128, 8192], P('seq', None, ('fsdp', 'sub')), may hold values from -0.09375 to 0.09375
Outputs:
- mixed: bfloat16 [8192, 8192], P(('groups', 'seq'), ('fsdp', 'sub')), parts along dimension 0
There are 2 independent parts, one for each index of `groups`. A program takes and returns all parts, laid end to end along the dimension named above; an argument that names none is the same for every part. Nothing has to cross between parts.
All inputs are finite; a program needn't handle non-finite values.
Results may differ from a plain program's by a relative error of at most 0.0084.
Values may be sent and summed in bfloat16 or wider, within the bound.
A program may use at most 64 MiB of HBM per device.

v0:
```python
import math

import jax
import jax.numpy as jnp
import numpy as np
from jax import lax
from jax.sharding import PartitionSpec as P

BLOCK = 512


def laid_out(pieces, dim):
    pieces = jnp.moveaxis(pieces, 0, dim)
    dims = pieces.shape
    return pieces.reshape(*dims[:dim], dims[dim] * dims[dim + 1], *dims[dim + 2 :])


def copy_for_each(array, axis):
    copies = jnp.broadcast_to(array, (lax.axis_size(axis), *array.shape))
    return lax.all_to_all(copies, axis, split_axis=0, concat_axis=0, tiled=True)


def gathered_copies(array, axis, dim):
    return laid_out(copy_for_each(array, axis), dim)


def taylor_first(vectors):
    feature_count = vectors.shape[0]
    first_row, second_row = np.triu_indices(feature_count, 1)
    cross_terms = vectors[first_row] * vectors[second_row] / 4.0
    squares = vectors * vectors / (4.0 * math.sqrt(2.0))
    leading = jnp.ones((1,) + vectors.shape[1:], jnp.float32)
    return jnp.concatenate([leading, vectors / 2.0, cross_terms, squares], 0)


def head_norm(numerator, head_gain, channel_axis):
    widened = numerator.astype(jnp.float32)
    meansq = jnp.mean(widened * widened, axis=channel_axis, keepdims=True)
    gain_shape = tuple((-1 if axis_pos == channel_axis else 1 for axis_pos in range(widened.ndim)))
    return (widened * lax.rsqrt(meansq + 1e-06) * head_gain.reshape(gain_shape)).astype(
        jnp.bfloat16
    )


def attend(queries, key_vectors, values_local):
    length = queries.shape[1]
    nblocks = length // BLOCK
    channels = values_local.shape[0]
    query_feats = taylor_first(queries.astype(jnp.float32)).astype(jnp.bfloat16)
    key_feats = taylor_first(key_vectors.astype(jnp.float32)).astype(jnp.bfloat16)
    taylor_width = query_feats.shape[0]
    contrib = jnp.einsum(
        "fbj,ebj->bfe",
        key_feats.reshape(taylor_width, nblocks, BLOCK),
        values_local.reshape(channels, nblocks, BLOCK),
        preferred_element_type=jnp.float32,
    )
    prefix = jnp.concatenate([jnp.zeros_like(contrib[:1]), jnp.cumsum(contrib[:-1], axis=0)], 0)
    prior_state = prefix.astype(jnp.bfloat16)
    carried = jnp.einsum(
        "bfe,fbt->bet",
        prior_state,
        query_feats.reshape(taylor_width, nblocks, BLOCK),
        preferred_element_type=jnp.float32,
    )
    earlier = lax.broadcasted_iota(jnp.int32, (BLOCK, BLOCK), 0)
    column_pos = lax.broadcasted_iota(jnp.int32, (BLOCK, BLOCK), 1)
    causal = earlier <= column_pos

    def one_block(block_index):
        offset = block_index * BLOCK
        query_block = lax.dynamic_slice_in_dim(queries, offset, BLOCK, 1)
        key_block = lax.dynamic_slice_in_dim(key_vectors, offset, BLOCK, 1)
        value_block = lax.dynamic_slice_in_dim(values_local, offset, BLOCK, 1)
        scores = jnp.einsum("fj,ft->jt", key_block, query_block, preferred_element_type=jnp.float32)
        kernel = 1.0 + scores / 4.0 + scores * scores / 32.0
        weight = jnp.where(causal, kernel, 0.0).astype(jnp.bfloat16)
        return jnp.einsum("ej,jt->et", value_block, weight, preferred_element_type=jnp.float32)

    local_part = lax.map(one_block, jnp.arange(nblocks, dtype=jnp.int32))
    numerator = (local_part + carried).astype(jnp.bfloat16)
    return jnp.transpose(numerator, (1, 0, 2)).reshape(channels, length)


def per_device(tokens, norm_gain, w_query, w_key, w_value, head_gain, w_out):
    feat_dev = w_query.shape[1]
    inputs = tokens.astype(jnp.float32)
    meansq = jnp.mean(inputs * inputs, axis=1, keepdims=True)
    normed = (inputs * lax.rsqrt(meansq + 1e-05) * norm_gain).astype(jnp.bfloat16)
    stacked = jnp.concatenate([w_query, w_key, w_value], 1)
    head_weights = lax.all_gather(stacked, "seq", axis=0, tiled=True)
    projected = jnp.einsum(
        "hcd,td->hct", head_weights, normed, preferred_element_type=jnp.float32
    ).astype(jnp.bfloat16)
    by_head = lax.all_to_all(projected, "seq", split_axis=0, concat_axis=2, tiled=True)
    qk_local = by_head[:, : 2 * feat_dev]
    values_local = by_head[0, 2 * feat_dev :]
    qk_whole = gathered_copies(qk_local, "fsdp", 0)
    length = qk_whole.shape[2]
    queries = qk_whole[:, :feat_dev].reshape(-1, length)
    key_vectors = qk_whole[:, feat_dev:].reshape(-1, length)
    numerator = attend(queries, key_vectors, values_local)
    out_weights = lax.all_gather(w_out, "seq", axis=0, tiled=True)
    heads_total = out_weights.shape[0]
    head_width = out_weights.shape[1]
    by_token = lax.all_to_all(numerator[None], "seq", split_axis=2, concat_axis=0, tiled=True)
    everyone = gathered_copies(by_token[None], ("fsdp", "sub"), 0)
    arranged = everyone.reshape(
        lax.axis_size("fsdp"),
        lax.axis_size("sub"),
        everyone.shape[1],
        everyone.shape[2],
        everyone.shape[3],
    )
    arranged = jnp.transpose(arranged, (2, 1, 0, 3, 4)).reshape(heads_total, head_width, -1)
    attended = head_norm(arranged, head_gain, 1)
    mixed = jnp.einsum("het,hed->td", attended, out_weights, preferred_element_type=jnp.float32)
    return mixed.astype(jnp.bfloat16)


def solution(mesh):
    in_specs = (
        P(("groups", "seq"), None),
        P(),
        P(("seq", "sub"), "fsdp", None),
        P(("seq", "sub"), "fsdp", None),
        P(("seq", "sub"), "fsdp", None),
        P(),
        P("seq", None, ("fsdp", "sub")),
    )
    out_specs = P(("groups", "seq"), ("fsdp", "sub"))
    return jax.shard_map(
        per_device, mesh=mesh, in_specs=in_specs, out_specs=out_specs, check_vma=False
    )
```

profile of v0, /device:TPU:65, one launch (start us, length us, event | category | flops | bytes accessed | tf_op | source)
XLA Modules:
  0.0 342.6 jit_solution(4627285938782507637)
XLA Ops:
  6.6 1.9 pad_maximum_fusion
  8.5 3.1 fusion.18
  11.7 119.0 %all-gather.3.cloned.1.call-done = bf16[16,20,8192]{2,1,0:T(8,128)(2,1)} async-done(((bf16[1,20,8192]{2,1,0:T(8,128)(2,1)}), bf16[16,20,8192]{2,1,0:T(8,128)(2,1)}) %all-gather.3.cloned.1.call-update) | async-done | bytes 5242896 | tf_op jit(solution)/shard_map/all_gather | solution.py:91
  130.6 6.7 %fusion.45 = bf16[16,20,256]{2,1,0:T(8,128)(2,1)} fusion(bf16[16,20,8192]{2,1,0:T(8,128)(2,1)} %all-gather.3.cloned.1.call-done, bf16[256,8192]{1,0:T(8,128)(2,1)} %param.17, f32[8192]{0:T(1024)S(1)} %copy-done.6, f32[256]{0:T(256)S(1)} %add_rsqrt_fusion), kind=kOutput, calls=%fused_computation.54 | convolution fusion | flops 1350647808 | bytes 9634816 | tf_op jit(solution)/shard_map/hcd,td->hct/dot_general | solution.py:92
  137.3 9.1 %all-to-all-start = ((bf16[16,20,256]{2,1,0:T(8,128)(2,1)}), bf16[16,20,256]{2,1,0:T(8,128)(2,1)S(1)}, u32[]{:S(2)}, u32[]{:S(2)}) async-start(bf16[16,20,256]{2,1,0:T(8,128)(2,1)} %fusion.45), calls=%async_computation | async-start | bytes 393216 | tf_op jit(solution)/shard_map/all_to_all | solution.py:95
  147.3 11.2 %all-to-all-done = bf16[16,20,256]{2,1,0:T(8,128)(2,1)S(1)} async-done(((bf16[16,20,256]{2,1,0:T(8,128)(2,1)}), bf16[16,20,256]{2,1,0:T(8,128)(2,1)S(1)}, u32[]{:S(2)}, u32[]{:S(2)}) %all-to-all-start) | async-done | bytes 163872 | tf_op jit(solution)/shard_map/all_to_all | solution.py:95
  159.4 6.4 %all-to-all-start.1 = ((bf16[8,1,4,4096]{3,2,1,0:T(4,128)(2,1)}), bf16[8,1,4,4096]{3,2,1,0:T(4,128)(2,1)S(1)}, u32[]{:S(2)}, u32[]{:S(2)}) async-start(bf16[8,1,4,4096]{3,2,1,0:T(4,128)(2,1)} %broadcast_in_dim.37), calls=%async_computation.1 | async-start | bytes 524288 | tf_op jit(solution)/shard_map/all_to_all | solution.py:20
  167.3 7.9 %all-to-all-done.1 = bf16[8,1,4,4096]{3,2,1,0:T(4,128)(2,1)S(1)} async-done(((bf16[8,1,4,4096]{3,2,1,0:T(4,128)(2,1)}), bf16[8,1,4,4096]{3,2,1,0:T(4,128)(2,1)S(1)}, u32[]{:S(2)}, u32[]{:S(2)}) %all-to-all-start.1) | async-done | bytes 262176 | tf_op jit(solution)/shard_map/all_to_all | solution.py:20
  175.4 1.4 fusion.62
  176.9 2.5 gather_fusion
  179.3 2.5 gather_fusion.1
  181.9 1.3 gather_fusion.2
  183.2 2.5 gather_fusion.3
  185.7 2.4 multiply_convert_fusion.3
  191.5 1.8 multiply_convert_fusion.2
  195.3 19.3 %while.11 = (s32[]{:T(128)}, f32[8,16,512]{2,1,0:T(8,128)S(1)}, s32[8]{0:T(128)S(1)}, bf16[16,4096]{1,0:T(8,128)(2,1)}, bf16[16,4096]{1,0:T(8,128)(2,1)S(1)}, /*...) while((s32[]{:T(128)}, f32[8,16,512]{2,1,0:T(8,128)S(1)}, ...), condition=%wide.region_2.3_spmd.clone, body=%wide.region_1.0_spmd.clone.sunk | while | flops 18874372 | bytes 84127 | solution.py:80
  196.5 1.2 fusion.81
  198.9 1.2 fusion.81
  201.4 1.2 fusion.81
  203.8 1.2 fusion.81
  206.2 1.2 fusion.81
  208.6 1.2 fusion.81
  211.0 1.2 fusion.81
  213.4 1.2 fusion.81
  215.3 2.7 copy.76
  218.5 22.6 %reduce.4 = bf16[4096,16]{1,0:T(8,128)(2,1)S(1)} reduce(bf16[4096,1,16]{2,1,0:T(2,128)(2,1)S(1)} %bitcast.70, bf16[]{:T(256)} %broadcast.136), dimensions={1}, to_apply=%bitcast.56.reduce_sub_computation | reduce | bytes 262146
  242.3 22.1 %all_to_all.43 = bf16[16,2,2048]{2,1,0:T(2,128)(2,1)S(1)} all-to-all(bf16[16,2,2048]{2,1,0:T(2,128)(2,1)S(1)} %reshape.133), channel_id=1, replica_groups=mesh['groups'=2,'seq'=16,'fsdp'=8,'sub'=2] {'seq'}, dimensions={0} | all-to-all | bytes 262144 | tf_op jit(solution)/shard_map/all_to_all | solution.py:106
  264.4 1.8 reshape.134
  266.2 2.0 copy.77
  268.5 57.5 %all_to_all.44 = bf16[16,1,16,16,256]{4,3,2,1,0:T(8,128)(2,1)S(1)} all-to-all(bf16[16,1,16,16,256]{4,3,2,1,0:T(8,128)(2,1)S(1)} %broadcast_in_dim.43), channel_id=1, replica_groups=mesh['groups'=2,'seq'=16,'fsdp'=8,'sub'=2] {'fsdp','sub'}, dimensions={0} | all-to-all | bytes 4194304 | tf_op jit(solution)/shard_map/all_to_all | solution.py:20
  326.6 2.6 copy.80
  330.2 5.5 %fusion.44 = bf16[256,512]{1,0:T(8,128)(2,1)} fusion(bf16[32,128,512]{2,1,0:T(8,128)(2,1)} %all-gather.5.cloned.1.call-done, f32[32,128,256]{2,1,0:T(8,128)} %bitcast.72, f32[128]{0:T(128)S(1)} %copy-done.7, f32[32,256]{1,0:T(8,128)S(1)} %rsqrt.21), kind=kOutput, calls=%fused_computation.53 | convolution fusion | flops 1077018624 | bytes 8684032 | tf_op jit(solution)/shard_map/het,hed->td/dot_general | solution.py:117
  (75 shorter events, 17.8 us)
Async XLA Ops:
  6.5 124.1 %copy-start.6 = (f32[8192]{0:T(1024)S(1)}, f32[8192]{0:T(1024)}, u32[]{:S(2)}) copy-start(f32[8192]{0:T(1024)} %param.18) | copy-start | bytes 98308
  6.5 124.1 %all-gather.3.cloned.1.call-start = ((), (), s32[]{:S(2)}) async-start(), calls=%async_computation.4 | async-start | bytes 6684672 | tf_op jit(solution)/shard_map/all_gather | solution.py:91
  11.6 135.6 %copy-start.5 = (s32[120]{0:T(128)S(1)}, s32[120]{0:T(128)}, u32[]{:S(2)}) copy-start(s32[120]{0:T(128)} %constant.78) | copy-start | bytes 1444
  11.6 135.6 %copy-start.4 = (s32[120]{0:T(128)S(1)}, s32[120]{0:T(128)}, u32[]{:S(2)}) copy-start(s32[120]{0:T(128)} %constant.79) | copy-start | bytes 1444
  137.3 21.2 %all-to-all-start = ((bf16[16,20,256]{2,1,0:T(8,128)(2,1)}), bf16[16,20,256]{2,1,0:T(8,128)(2,1)S(1)}, u32[]{:S(2)}, u32[]{:S(2)}) async-start(bf16[16,20,256]{2,1,0:T(8,128)(2,1)} %fusion.45), calls=%async_computation | async-start | bytes 393216 | tf_op jit(solution)/shard_map/all_to_all | solution.py:95
  146.4 183.8 %all-gather.5.cloned.1.call-start = ((), (), s32[]{:S(2)}) async-start(), calls=%async_computation.5 | async-start | bytes 4456448 | tf_op jit(solution)/shard_map/all_gather | solution.py:103
  159.4 15.8 %all-to-all-start.1 = ((bf16[8,1,4,4096]{3,2,1,0:T(4,128)(2,1)}), bf16[8,1,4,4096]{3,2,1,0:T(4,128)(2,1)S(1)}, u32[]{:S(2)}, u32[]{:S(2)}) async-start(bf16[8,1,4,4096]{3,2,1,0:T(4,128)(2,1)} %broadcast_in_dim.37), calls=%async_computation.1 | async-start | bytes 524288 | tf_op jit(solution)/shard_map/all_to_all | solution.py:20
  191.5 1.9 copy-start
  193.3 0.9 copy-start.1
  193.3 1.0 copy-start.2
  193.3 1.0 copy-start.3
  194.3 0.9 copy-start.8
  329.2 1.0 copy-start.7
Sparse Core Ops, SparseCore 0:
  9.4 121.1 all-gather.2
  149.3 71.7 all-gather.4
where the time goes:
time: 344 us; the launch traced here: 343 us
  waiting for transfers between devices  139 us (40%)
  blocking collectives  79.6 us (23%)
  other arithmetic  34.7 us (10%)
  local copies, waits for them, and re-layouts  32.1 us (9%)
  matrix products  22.6 us (7%)
  starting transfers between devices  15.6 us (5%)
  between operations  13.8 us (4%)
  loops' own time  5.26 us (2%)
    all_gather x1, waiting for transfers between devices, per_device(): head_weights = lax.all_gather(stacked, 'seq', axis=0, tiled=True)  119 us
    all_to_all x1, blocking collectives, copy_for_each(): return lax.all_to_all(copies, axis, split_axis=0, concat_axis=0, tiled=True)  57.5 us
    unnamed x1, other arithmetic  22.6 us
    all_to_all x1, blocking collectives, per_device(): lax.all_to_all(numerator[None], 'seq', split_axis=2, concat_axis=0, tiled...  22.1 us
    all_to_all x1, waiting for transfers between devices, per_device(): lax.all_to_all(projected, 'seq', split_axis=0, concat_axis=2, tiled=True)  11.2 us
    dot_general x8, matrix products, one_block(): jnp.einsum('ej,jt->et', value_block, weight, preferred_element_type=jnp.f...  9.3 us
    all_to_all x1, starting transfers between devices, per_device(): lax.all_to_all(projected, 'seq', split_axis=0, concat_axis=2, tiled=True)  9.07 us
    gather x4, local copies, waits for them, and re-layouts, taylor_first(): cross_terms = vectors[first_row] * vectors[second_row] / 4.0  8.71 us
  transfers between devices with their start and end apart: 4, of which 3 were waited for; matrix products, arithmetic and copies ran while one was open for 22% of the time, Pallas kernels for 0%

commit v1 on v0

v1 whole, which is shorter than its diff:
```python
import functools

import jax
import jax.numpy as jnp
import numpy as np
from jax import lax
from jax.experimental import pallas as pl
from jax.experimental.pallas import tpu as pltpu
from jax.sharding import PartitionSpec as P

BLOCK = 512
LANES = 128
STATE_ROWS = 160
MESH = pl.DeviceIdType.MESH
bf16, f32 = jnp.bfloat16, jnp.float32


def feature_tables(owners, dims):
    count = owners * dims
    tables = np.zeros((2, 4, LANES, 2 * LANES), np.float32)
    bias = np.zeros((8, 2 * LANES), np.float32)
    for head in range(2):
        for kind in range(2):

            def entry(i):
                return (i // dims) * 4 * dims + head * 2 * dims + kind * dims + i % dims

            first, second = tables[head, 2 * kind], tables[head, 2 * kind + 1]
            for i in range(count):
                first[entry(i), i] = 0.5
            column = count + 1
            for i in range(count):
                for j in range(i, count):
                    first[entry(i), column] = 0.125 if (i == j and kind == 1) else 0.25
                    second[entry(j), column] = 1.0
                    column += 1
    bias[0, count] = 1.0
    bias[1, : count + 1] = 1.0
    return jnp.asarray(tables, bf16), jnp.asarray(bias, f32)


class Ring:
    def __init__(self, axis, size, me, piece, pieces, split, send, recv):
        self.axis, self.size, self.me = axis, size, me
        self.piece, self.pieces, self.split = piece, pieces, split
        self.send, self.recv, self.last = send, recv, size // 2

    def moves(self, way, step, p):
        return step < self.last or (p < self.split) == (way == 0)

    def block(self, way, back):
        return lax.rem(self.me + (self.size - back if way == 0 else back), self.size)

    def copy(self, way, step, p, block):
        to = lax.rem(self.me + (1 if way == 0 else self.size - 1), self.size)
        ref = self.piece(p, block)
        return pltpu.make_async_remote_copy(
            src_ref=ref,
            dst_ref=ref,
            send_sem=self.send.at[way, step - 1, p],
            recv_sem=self.recv.at[way, step - 1, p],
            device_id={self.axis: to},
            device_id_type=MESH,
        )

    def start(self, way, step, p):
        if step <= self.last and self.moves(way, step, p):
            self.copy(way, step, p, self.block(way, step - 1)).start()

    def first(self):
        for p in range(self.pieces):
            for way in range(2):
                self.start(way, 1, p)

    def tick(self, step, arrived=None):
        for p in range(self.pieces):
            for way in range(2):
                if self.moves(way, step, p):
                    self.copy(way, step, p, self.block(way, step)).wait_recv()
                    self.start(way, step + 1, p)
                    if arrived is not None:
                        arrived(way, step, p, self.block(way, step))

    def drain(self):
        for step in range(1, self.last + 1):
            for p in range(self.pieces):
                for way in range(2):
                    if self.moves(way, step, p):
                        self.copy(way, step, p, self.me).wait_send()


def nt(a, b):
    return lax.dot_general(a, b, (((1,), (1,)), ((), ())), preferred_element_type=f32)


def layer(S, X, tokens, gain, wq, wk, wv, hgain, wo, tab, bias, out,
          tokv, T, W, QKf, qkown, qkin, Pm, Rcv, Snd, Rx, tabv, Cown, Crecv, Sacc, Sp, num, A0, A1, Att, WO, acc,
          lsem, tS, tR, wS, wR, oS, oR, aS, aR, pS, pR, e2S, e2R, e3S, e3R, cS, cR, e4S, e4R, zS, zR, ownS, ownR, relS, relR):
    x, z, c = lax.axis_index("fsdp"), lax.axis_index("seq"), lax.axis_index("sub")
    R, D = tokv.shape
    Dh = D // 2
    vd, fd = wv.shape[0], wq.shape[0]
    HD = X * vd
    PB, Ppl = Rx.shape[0], Rx.shape[1]
    Bk = PB * Ppl
    other = 1 - c
    mine = pl.ds(pl.multiple_of(c * Dh, LANES), Dh)
    theirs = pl.ds(pl.multiple_of(other * Dh, LANES), Dh)

    def rows(i, n):
        return pl.ds(pl.multiple_of(i * n, n), n)

    def remote(src, dst, send, recv, **device):
        return pltpu.make_async_remote_copy(
            src_ref=src, dst_ref=dst, send_sem=send, recv_sem=recv, device_id=device, device_id_type=MESH)

    barrier = pltpu.get_barrier_semaphore()
    for k in range(1, S):
        pl.semaphore_signal(barrier, inc=1, device_id={"seq": lax.rem(z + k, S)}, device_id_type=MESH)
    for k in range(1, X):
        pl.semaphore_signal(barrier, inc=1, device_id={"fsdp": lax.rem(x + k, X)}, device_id_type=MESH)
    pl.semaphore_signal(barrier, inc=1, device_id={"sub": other}, device_id_type=MESH)

    get_tokens = pltpu.make_async_copy(tokens.at[rows(x, R)], tokv, lsem.at[0])
    get_value = pltpu.make_async_copy(wv.at[:, mine], W.at[rows(x, vd)], lsem.at[1])
    get_out = pltpu.make_async_copy(wo, WO.at[z], lsem.at[2])
    get_tab = pltpu.make_async_copy(tab.at[c], tabv, lsem.at[3])
    get_tokens.start()
    get_value.start()
    get_out.start()
    get_tab.start()

    W[2 * HD + 4 * fd * X :, :] = jnp.zeros((W.shape[0] - 2 * HD - 4 * fd * X, Dh), bf16)
    qkown[...] = jnp.zeros_like(qkown)
    for head in range(2):
        @pl.when(c == head)
        def _():
            base = 2 * fd * head
            qkown[base : base + fd, :] = wq[...].astype(f32)
            qkown[base + fd : base + 2 * fd, :] = wk[...].astype(f32)

    get_tokens.wait()
    chunk = min(1024, D)

    def squares(i, total):
        part = tokv[:, pl.ds(pl.multiple_of(i * chunk, chunk), chunk)].astype(f32)
        return total + jnp.sum(part * part, axis=1, keepdims=True)

    meansq = lax.fori_loop(0, D // chunk, squares, jnp.zeros((R, 1), f32)) / D
    scale = lax.rsqrt(meansq + 1e-05)
    chunk = min(1024, Dh)

    @pl.loop(0, Dh // chunk)
    def _(i):
        here = pl.ds(pl.multiple_of(c * Dh + i * chunk, chunk), chunk)
        part = tokv[:, here].astype(f32) * scale * gain[:, here]
        T[z, :, pl.ds(pl.multiple_of(i * chunk, chunk), chunk)] = part.astype(bf16)

    pl.semaphore_wait(barrier, S + X - 1)

    half = R // 2
    token_ring = Ring("seq", S, z, lambda p, b: T.at[b, half * p : half * (p + 1)], 2, 1, tS, tR)
    token_ring.first()

    give_value = remote(wv.at[:, theirs], W.at[pl.ds(pl.multiple_of(HD + x * vd, vd), vd)], pS.at[0], pR.at[0], sub=other)
    give_qk = remote(qkown.at[:, theirs], qkin, pS.at[1], pR.at[1], sub=other)
    give_value.start()
    give_qk.start()

    def weight_piece(p, b):
        if p == 2:
            return QKf.at[rows(b, 4 * fd)]
        return W.at[pl.ds(pl.multiple_of(HD * p + b * vd, vd), vd)]

    weight_ring = Ring("fsdp", X, x, weight_piece, 3, 1, wS, wR)
    get_value.wait()
    give_value.wait_recv()
    give_qk.wait_recv()
    QKf[rows(x, 4 * fd), :] = qkown[:, mine] + qkin[...]
    weight_ring.first()

    Oh = 2 * HD // 2
    out_ring = Ring("seq", S, z, lambda p, b: WO.at[b, Oh * p : Oh * (p + 1)], 2, 1, oS, oR)

    ticks = [(5.6 * s, 0, s) for s in range(1, S // 2 + 1)] + [(3.0 + 8.5 * s, 1, s) for s in range(1, X // 2 + 1)]
    for _, which, step in sorted(ticks):
        if which == 0:
            if step == S // 2:
                get_out.wait()
                out_ring.first()
            token_ring.tick(step)
        else:
            weight_ring.tick(step)

    W[2 * HD : 2 * HD + 4 * fd * X, :] = QKf[...].astype(bf16)
    group = min(4, S)

    @pl.loop(0, S // group)
    def _(i):
        lhs = T[pl.ds(i * group, group)].reshape(group * R, Dh)
        Pm[rows(i, group * R), :] = nt(lhs, W[...])

    swap = remote(Pm.at[:, HD : 2 * HD + LANES], Rcv, e2S.at[0], e2R.at[0], sub=other)
    swap.start()
    get_tab.wait()
    swap.wait_recv()
    Snd[:, :, :HD] = (Pm[:, :HD] + Rcv[:, :HD]).astype(bf16).reshape(S, R, HD)
    Snd[:, :, HD:] = (Pm[:, 2 * HD :] + Rcv[:, HD:]).astype(bf16).reshape(S, R, LANES)

    def to_block(k):
        to = lax.rem(x + k, X)
        return remote(Snd.at[pl.ds(to * PB, PB)], Rx.at[:, rows(x, R)], e3S.at[k], e3R.at[k], fsdp=to)

    for k in range(1, X):
        to_block(k).start()
    Rx[:, rows(x, R), :] = Snd[pl.ds(x * PB, PB)]
    out_ring.tick(1)
    for k in range(1, X):
        to_block(k).wait_recv()

    val = Rx[:, :, :HD].reshape(Bk, HD)
    qk = Rx[:, :, HD:].reshape(Bk, LANES)

    def factor(which):
        return jnp.dot(qk, tabv[which], preferred_element_type=f32)

    b1, b2 = bias[0:1, :], bias[1:2, :]
    key_feats = ((factor(2) + b1) * (factor(3) + b2)).astype(bf16)
    contrib = lax.dot_general(key_feats, val, (((0,), (0,)), ((), ())), preferred_element_type=f32)
    Cown[...] = contrib[:STATE_ROWS].astype(bf16)

    def to_later(k):
        return remote(Cown, Crecv.at[k], cS.at[k], cR.at[k], fsdp=lax.rem(x + k, X))

    for k in range(1, X):
        @pl.when(x + k < X)
        def _():
            to_later(k).start()

    query_feats = ((factor(0) + b1) * (factor(1) + b2)).astype(bf16)
    lane = lax.broadcasted_iota(jnp.int32, (Bk, LANES), 1)
    count = X * fd
    zero = jnp.zeros((Bk, LANES), bf16)
    line_q = jnp.where(lane <= count, query_feats[:, :LANES], zero)
    line_k = jnp.where(lane <= count, key_feats[:, :LANES], zero)
    tile = min(128, Bk)
    for i in range(Bk // tile):
        seen = (i + 1) * tile
        g = nt(line_q[i * tile : seen], line_k[:seen])
        at = i * tile + lax.broadcasted_iota(jnp.int32, (tile, seen), 0)
        key_at = lax.broadcasted_iota(jnp.int32, (tile, seen), 1)
        weight = jnp.where(key_at <= at, 0.5 * (g * g) + 0.5, 0.0).astype(bf16)
        num[i * tile : seen, :] = jnp.dot(weight, val[:seen], preferred_element_type=f32)

    Sacc[...] = jnp.zeros_like(Sacc)
    for k in range(1, X):
        @pl.when(x >= k)
        def _():
            to_later(k).wait_recv()
            Sacc[...] += Crecv[k].astype(f32)

    Sp[STATE_ROWS:, :] = jnp.zeros((2 * LANES - STATE_ROWS, HD), bf16)
    Sp[:STATE_ROWS, :] = Sacc[...].astype(bf16)
    numerator = num[...] + jnp.dot(query_feats, Sp[...], preferred_element_type=f32)
    widened = numerator.astype(bf16).astype(f32)
    power = jnp.mean(widened * widened, axis=1, keepdims=True)
    attended = (widened * lax.rsqrt(power + 1e-06) * hgain[...]).astype(bf16)
    A0[...] = attended.reshape(PB, Ppl, HD)

    def to_share(k):
        to = lax.rem(x + k, X)
        return remote(A0.at[:, rows(to, R)], A1.at[pl.ds(x * PB, PB)], e4S.at[k], e4R.at[k], fsdp=to)

    for k in range(1, X):
        to_share(k).start()
    A1[pl.ds(x * PB, PB)] = A0[:, rows(x, R), :]
    out_ring.tick(2)
    for k in range(1, X):
        to_share(k).wait_recv()

    lanes = pl.ds(pl.multiple_of(c * HD, LANES), HD)

    def to_plane(k):
        to = lax.rem(z + k, S)
        return remote(A1.at[to], Att.at[z, rows(x, R), lanes], zS.at[k], zR.at[k], seq=to)

    for k in range(1, S):
        to_plane(k).start()
    Att[z, rows(x, R), lanes] = A1[z]
    for step in range(3, S // 2 - 3):
        out_ring.tick(step)
    for k in range(1, S):
        to_plane(k).wait_recv()

    upper = S // 2

    def share(p, b):
        return Att.at[upper * p : upper * (p + 1), rows(b, R), lanes]

    def relay(way, step, p, b):
        return remote(share(p, b), share(p, b), relS.at[way, step - 1, p], relR.at[way, step - 1, p], sub=other)

    def own_relay(p):
        return remote(share(p, x), share(p, x), ownS.at[p], ownR.at[p], sub=other)

    share_ring = Ring("fsdp", X, x, share, 2, 1, aS, aR)
    share_ring.first()
    for p in range(2):
        own_relay(p).start()
    done = max(S // 2 - 4, 2)
    for step in range(1, X // 2 + 1):
        share_ring.tick(step, lambda way, s, p, b: relay(way, s, p, b).start())
        if step == 2 and S // 2 > 4:
            done += 1
            out_ring.tick(done)

    other_lanes = pl.ds(pl.multiple_of(other * HD, LANES), HD)
    for p in range(2):
        own_relay(p).wait_recv()
    for step in range(1, X // 2 + 1):
        for p in range(2):
            for way in range(2):
                if share_ring.moves(way, step, p):
                    relay(way, step, p, share_ring.block(way, step)).wait_recv()

    acc[...] = jnp.dot(Att[z], WO[z], preferred_element_type=f32)

    def add(b):
        acc[...] += jnp.dot(Att[b], WO[b], preferred_element_type=f32)

    @pl.loop(1, done + 1)
    def _(s):
        add(lax.rem(z + s, S))

        @pl.when(s < S // 2)
        def _():
            add(lax.rem(z + S - s, S))

    for step in range(done + 1, S // 2 + 1):
        out_ring.tick(step)
        add(lax.rem(z + step, S))
        if step < S // 2:
            add(lax.rem(z + S - step, S))
    out[...] = acc[...].astype(bf16)

    token_ring.drain()
    weight_ring.drain()
    out_ring.drain()
    share_ring.drain()
    give_value.wait_send()
    give_qk.wait_send()
    swap.wait_send()
    for k in range(1, X):
        to_block(k).wait_send()
        to_share(k).wait_send()

        @pl.when(x + k < X)
        def _():
            to_later(k).wait_send()
    for k in range(1, S):
        to_plane(k).wait_send()
    for p in range(2):
        own_relay(p).wait_send()
    for step in range(1, X // 2 + 1):
        for p in range(2):
            for way in range(2):
                if share_ring.moves(way, step, p):
                    relay(way, step, p, x).wait_send()


def solution(mesh):
    S, X = mesh.shape["seq"], mesh.shape["fsdp"]

    def per_device(tokens, norm_gain, w_query, w_key, w_value, head_gain, w_out):
        Ppl, D = tokens.shape
        fd, vd = w_query.shape[1], w_value.shape[1]
        HD, R, Dh, C = X * vd, Ppl // X, D // 2, w_out.shape[2]
        PB = BLOCK // Ppl
        tab, bias = feature_tables(X, fd)
        any_ref = pl.BlockSpec(memory_space=pl.ANY)
        vm = pl.BlockSpec(memory_space=pltpu.VMEM)
        dma = pltpu.SemaphoreType.DMA
        V = pltpu.VMEM
        scratch = [
            V((R, D), bf16),
            V((S, R, Dh), bf16),
            V((2 * HD + LANES, Dh), bf16),
            V((4 * fd * X, Dh), f32),
            V((4 * fd, D), f32),
            V((4 * fd, Dh), f32),
            V((S * R, 2 * HD + LANES), f32),
            V((S * R, HD + LANES), f32),
            V((S, R, HD + LANES), bf16),
            V((PB, Ppl, HD + LANES), bf16),
            V((4, LANES, 2 * LANES), bf16),
            V((STATE_ROWS, HD), bf16),
            V((X, STATE_ROWS, HD), bf16),
            V((STATE_ROWS, HD), f32),
            V((2 * LANES, HD), bf16),
            V((PB * Ppl, HD), f32),
            V((PB, Ppl, HD), bf16),
            V((S, R, HD), bf16),
            V((S, Ppl, 2 * HD), bf16),
            V((S, 2 * HD, C), bf16),
            V((Ppl, C), f32),
            dma((4,)),
            dma((2, S // 2, 2)), dma((2, S // 2, 2)),
            dma((2, X // 2, 3)), dma((2, X // 2, 3)),
            dma((2, S // 2, 2)), dma((2, S // 2, 2)),
            dma((2, X // 2, 2)), dma((2, X // 2, 2)),
            dma((2,)), dma((2,)),
            dma((1,)), dma((1,)),
            dma((X,)), dma((X,)),
            dma((X,)), dma((X,)),
            dma((X,)), dma((X,)),
            dma((S,)), dma((S,)),
            dma((2,)), dma((2,)),
            dma((2, X // 2, 2)), dma((2, X // 2, 2)),
        ]
        return pl.pallas_call(
            functools.partial(layer, S, X),
            out_shape=jax.ShapeDtypeStruct((Ppl, C), bf16),
            in_specs=[any_ref, vm, vm, vm, any_ref, vm, any_ref, any_ref, vm],
            out_specs=vm,
            scratch_shapes=scratch,
            compiler_params=pltpu.CompilerParams(
                collective_id=0, has_side_effects=True, vmem_limit_bytes=48 * 1024 * 1024),
            name="layer",
        )(
            tokens,
            norm_gain.reshape(1, D),
            w_query.reshape(fd, D),
            w_key.reshape(fd, D),
            w_value.reshape(vd, D),
            head_gain.reshape(1, HD),
            w_out.reshape(2 * HD, C),
            tab,
            bias,
        )

    in_specs = (
        P(("groups", "seq"), None),
        P(),
        P(("seq", "sub"), "fsdp", None),
        P(("seq", "sub"), "fsdp", None),
        P(("seq", "sub"), "fsdp", None),
        P(),
        P("seq", None, ("fsdp", "sub")),
    )
    out_specs = P(("groups", "seq"), ("fsdp", "sub"))
    return jax.shard_map(
        per_device, mesh=mesh, in_specs=in_specs, out_specs=out_specs, check_vma=False
    )
```

time: 344 us -> 189 us (0.55)
  Pallas kernels: 0 us -> 179 us
  waiting for transfers between devices: 139 us -> 0 us
  blocking collectives: 79.6 us -> 0 us
  other arithmetic: 34.7 us -> 0 us
  local copies, waits for them, and re-layouts: 32.1 us -> 9.46 us
  matrix products: 22.6 us -> 0 us
  starting transfers between devices: 15.6 us -> 0 us
  between operations: 13.8 us -> 0.02 us
  loops' own time: 5.26 us -> 0 us
    pallas_call x0 -> x1, Pallas kernels: none -> 179 us  [per_device(): pl.pallas_call(functools.partial(layer, S, X), out_shape=jax.ShapeDtypeSt...]
    all_gather x2 -> x0, waiting for transfers between devices: 119 us -> none  [the longest x1 119 us: per_device(): head_weights = lax.all_gather(stacked, 'seq', axis=0, tiled=True)]
    all_to_all x2 -> x0, blocking collectives: 79.6 us -> none  [the longest x1 57.5 us: copy_for_each(): return lax.all_to_all(copies, axis, split_axis=0, concat_axis=0, tiled=True)]
    unnamed x1 -> x0, other arithmetic: 22.6 us -> none
    dot_general x11 -> x0, matrix products: 22.1 us -> none  [the longest x8 9.3 us: one_block(): jnp.einsum('ej,jt->et', value_block, weight, preferred_element_type=jnp.f...]
    all_to_all x2 -> x0, waiting for transfers between devices: 19.2 us -> none  [the longest x1 11.2 us: per_device(): lax.all_to_all(projected, 'seq', split_axis=0, concat_axis=2, tiled=True)]
    all_to_all x2 -> x0, starting transfers between devices: 15.5 us -> none  [the longest x1 9.07 us: per_device(): lax.all_to_all(projected, 'seq', split_axis=0, concat_axis=2, tiled=True)]
    gather x4 -> x0, local copies, waits for them, and re-layouts: 8.71 us -> none  [taylor_first(): cross_terms = vectors[first_row] * vectors[second_row] / 4.0]
  transfers between devices with their start and end apart: 4 -> 0, of which waited for: 3 -> 0; matrix products, arithmetic and copies ran while one was open for 22% -> 0% of each run, Pallas kernels for 0% -> 0%
where the time goes in v1:
time: 189 us
  Pallas kernels  179 us (95%)
  local copies, waits for them, and re-layouts  9.46 us (5%)
    pallas_call x1, Pallas kernels, per_device(): pl.pallas_call(functools.partial(layer, S, X), out_shape=jax.ShapeDtypeSt...  179 us
    unnamed x19, local copies, waits for them, and re-layouts  9.46 us

profile of v1, /device:TPU:65, one launch (start us, length us, event | category | flops | bytes accessed | tf_op | source)
XLA Modules:
  0.0 188.8 jit_solution(17320836778214780038)
XLA Ops:
  0.0 0.0 copy-start
  0.0 2.2 %copy-done = bf16[256,8192]{1,0:T(8,128)(2,1)S(1)} copy-done((bf16[256,8192]{1,0:T(8,128)(2,1)S(1)}, bf16[256,8192]{1,0:T(8,128)(2,1)}, u32[]{:S(2)}) %copy-start) | copy-done | bytes 4194328
  2.2 0.0 copy-start.1
  2.2 1.0 copy-done.1
  3.2 0.0 copy-start.2
  3.2 0.9 copy-done.2
  4.2 0.0 copy-start.3
  4.2 0.9 copy-done.3
  5.1 0.0 copy-start.4
  5.1 0.8 copy-done.4
  5.9 0.0 copy-start.5
  5.9 0.8 copy-done.5
  6.6 0.0 copy-start.6
  6.7 0.8 copy-done.6
  7.4 0.0 copy-start.7
  7.4 0.7 copy-done.7
  8.1 0.0 copy-start.8
  8.1 0.7 copy-done.8
  8.8 179.3 %layer.1 = bf16[256,512]{1,0:T(8,128)(2,1)S(1)} custom-call(bf16[256,8192]{1,0:T(8,128)(2,1)S(1)} %copy-done, f32[1,8192]{1,0:T(1,128)S(1)} %bitcast.8, bf16[2,8192]{1,0:T(2,128)(2,1)S(1)} %bitcast.9, bf16[2,8192]{1,0:T(2,128)(2,1)S(1)} %bitcast.10, bf16[16,8192]{1,0:T(8,128)(2,1)S(1)} %bitcast.6, f32[1,128]{1,0:T(1,128)S(1)} %bitcast.11, ...), custom_call_target="tpu_custom_call" | custom-call | tf_op jit(solution)/shard_map/layer/pallas_call | solution.py:420
  188.1 0.7 copy.11
Async XLA Ops:
  0.0 2.2 %copy-start = (bf16[256,8192]{1,0:T(8,128)(2,1)S(1)}, bf16[256,8192]{1,0:T(8,128)(2,1)}, u32[]{:S(2)}) copy-start(bf16[256,8192]{1,0:T(8,128)(2,1)} %tokens.1) | copy-start | bytes 12582916
  2.2 1.0 copy-start.1
  3.2 0.9 copy-start.2
  4.2 0.9 copy-start.3
  5.1 0.8 copy-start.4
  5.9 0.8 copy-start.5
  6.6 0.8 copy-start.6
  7.4 0.7 copy-start.7
  8.1 0.7 copy-start.8

commit v2 on v1

v2 whole, which is shorter than its diff:
```python
import functools

import jax
import jax.numpy as jnp
import numpy as np
from jax import lax
from jax.experimental import pallas as pl
from jax.experimental.pallas import tpu as pltpu
from jax.sharding import PartitionSpec as P

LANES = 128
FEATURES = 160
GROUP = 4
MESH = pl.DeviceIdType.MESH
bf16, f32 = jnp.bfloat16, jnp.float32


def feature_tables(owners, dims):
    count = owners * dims
    queries = np.zeros((2, 2, LANES, 2 * LANES), np.float32)
    pick = np.zeros((2, count, 4 * count), np.float32)
    keys = np.zeros((2, FEATURES, count), np.float32)
    bias = np.zeros((8, 2 * LANES), np.float32)

    def entry(i, head, kind):
        return (i // dims) * 4 * dims + head * 2 * dims + kind * dims + i % dims

    for i in range(count):
        keys[0, i, i] = 0.5
        for head in range(2):
            queries[head, 0, entry(i, head, 0), i] = 0.5
            pick[head, i, entry(i, head, 1)] = 1.0
    feature = count + 1
    for i in range(count):
        for j in range(i, count):
            keys[0, feature, i] = 0.125 if i == j else 0.25
            keys[1, feature, j] = 1.0
            for head in range(2):
                queries[head, 0, entry(i, head, 0), feature] = 0.25
                queries[head, 1, entry(j, head, 0), feature] = 1.0
            feature += 1
    bias[0, count] = 1.0
    bias[1, : count + 1] = 1.0
    upright = np.zeros((2, FEATURES, LANES), np.float32)
    upright[0], upright[1] = bias[0, :FEATURES, None], bias[1, :FEATURES, None]
    return (jnp.asarray(queries, bf16), jnp.asarray(pick, bf16), jnp.asarray(keys, bf16),
            jnp.asarray(bias, f32), jnp.asarray(upright, f32))


class Ring:
    def __init__(self, axis, size, me, piece, pieces, split, send, recv):
        self.axis, self.size, self.me = axis, size, me
        self.piece, self.pieces, self.split = piece, pieces, split
        self.send, self.recv, self.last = send, recv, size // 2

    def moves(self, way, step, p):
        return step < self.last or (p < self.split) == (way == 0)

    def block(self, way, back):
        return lax.rem(self.me + (self.size - back if way == 0 else back), self.size)

    def copy(self, way, step, p, src, dst):
        to = lax.rem(self.me + (1 if way == 0 else self.size - 1), self.size)
        return pltpu.make_async_remote_copy(
            src_ref=src,
            dst_ref=dst,
            send_sem=self.send.at[way, step - 1, p],
            recv_sem=self.recv.at[way, step - 1, p],
            device_id={self.axis: to},
            device_id_type=MESH,
        )

    def start(self, way, step, p):
        if step <= self.last and self.moves(way, step, p):
            block = self.block(way, step - 1)
            self.copy(way, step, p, self.piece(p, way, step - 1, block), self.piece(p, way, step, block)).start()

    def first(self, pieces=None):
        for p in range(self.pieces) if pieces is None else pieces:
            for way in range(2):
                self.start(way, 1, p)

    def tick(self, step, arrived=None):
        for p in range(self.pieces):
            for way in range(2):
                if self.moves(way, step, p):
                    block = self.block(way, step)
                    ref = self.piece(p, way, step, block)
                    self.copy(way, step, p, ref, ref).wait_recv()
                    self.start(way, step + 1, p)
                    if arrived is not None:
                        arrived(way, step, p, block)

    def drain(self):
        for step in range(1, self.last + 1):
            for p in range(self.pieces):
                for way in range(2):
                    if self.moves(way, step, p):
                        ref = self.piece(p, way, step - 1, self.me)
                        self.copy(way, step, p, ref, ref).wait_send()


def nt(a, b):
    return lax.dot_general(a, b, (((1,), (1,)), ((), ())), preferred_element_type=f32)


def mm(a, b):
    return jnp.dot(a, b, preferred_element_type=f32)


def slot_of(size, way, step):
    if step == 0:
        return 0
    return size - 1 if step == size // 2 else 2 * step - 1 + way


def layer(S, X, sets, tokens, gain, wq, wk, wv, hgain, wo, qtab, pick, ktab, bias, upright, out,
          tokv, T, W, QKf, qkown, qkin, Pn, Rn, PT, RT, Qn, Vp, Kg, VBD, Cs, Sg, Fq, num, A1, Att, WO, acc, qtabv, pickv,
          lsem, tS, tR, wS, wR, oS, oR, aS, aR, kS, kR, pS, pR, e2S, e2R, zS, zR, ownS, ownR, relS, relR):
    x, z, c = lax.axis_index("fsdp"), lax.axis_index("seq"), lax.axis_index("sub")
    R, D = tokv.shape
    Dh = D // 2
    vd, fd = wv.shape[0], wq.shape[0]
    HD = X * vd
    count = X * fd
    other = 1 - c
    mine = pl.ds(pl.multiple_of(c * Dh, LANES), Dh)
    theirs = pl.ds(pl.multiple_of(other * Dh, LANES), Dh)

    def rows(i, n):
        return pl.ds(pl.multiple_of(i * n, n), n)

    def remote(src, dst, send, recv, **device):
        return pltpu.make_async_remote_copy(
            src_ref=src, dst_ref=dst, send_sem=send, recv_sem=recv, device_id=device, device_id_type=MESH)

    barrier = pltpu.get_barrier_semaphore()
    greeted = [{"seq": lax.rem(z + 1, S)}, {"seq": lax.rem(z + S - 1, S)}]
    greeted += [{"fsdp": lax.rem(x + 1, X)}, {"fsdp": lax.rem(x + X - 1, X)}, {"sub": other}]
    for device in greeted:
        pl.semaphore_signal(barrier, inc=1, device_id=device, device_id_type=MESH)

    get_tokens = pltpu.make_async_copy(tokens.at[rows(x, R)], tokv, lsem.at[0])
    get_value = pltpu.make_async_copy(wv.at[:, mine], W.at[rows(x, vd)], lsem.at[1])
    get_out = pltpu.make_async_copy(wo, WO.at[0], lsem.at[2])
    get_tab = pltpu.make_async_copy(qtab.at[c], qtabv, lsem.at[3])
    get_pick = pltpu.make_async_copy(pick.at[c], pickv, lsem.at[4])
    get_tokens.start()
    get_value.start()
    get_out.start()
    get_tab.start()
    get_pick.start()

    qkown[...] = jnp.zeros_like(qkown)
    for head in range(2):
        @pl.when(c == head)
        def _():
            base = 2 * fd * head
            qkown[base : base + fd, :] = wq[...].astype(f32)
            qkown[base + fd : base + 2 * fd, :] = wk[...].astype(f32)

    get_tokens.wait()
    chunk = min(1024, D)

    def squares(i, total):
        part = tokv[:, pl.ds(pl.multiple_of(i * chunk, chunk), chunk)].astype(f32)
        return total + jnp.sum(part * part, axis=1, keepdims=True)

    meansq = lax.fori_loop(0, D // chunk, squares, jnp.zeros((R, 1), f32)) / D
    scale = lax.rsqrt(meansq + 1e-05)
    chunk = min(1024, Dh)

    @pl.loop(0, Dh // chunk)
    def _(i):
        here = pl.ds(pl.multiple_of(c * Dh + i * chunk, chunk), chunk)
        part = tokv[:, here].astype(f32) * scale * gain[:, here]
        T[0, :, pl.ds(pl.multiple_of(i * chunk, chunk), chunk)] = part.astype(bf16)

    pl.semaphore_wait(barrier, len(greeted))

    half = R // 2
    token_ring = Ring("seq", S, z, lambda p, way, step, b: T.at[slot_of(S, way, step), half * p : half * (p + 1)], 2, 1, tS, tR)
    token_ring.first()

    give_value = remote(wv.at[:, theirs], W.at[pl.ds(pl.multiple_of(HD + x * vd, vd), vd)], pS.at[0], pR.at[0], sub=other)
    give_qk = remote(qkown.at[:, theirs], qkin, pS.at[1], pR.at[1], sub=other)
    give_value.start()
    give_qk.start()

    def weight_piece(p, way, step, b):
        if p == 2:
            return QKf.at[rows(b, 4 * fd)]
        return W.at[pl.ds(pl.multiple_of(HD * p + b * vd, vd), vd)]

    weight_ring = Ring("fsdp", X, x, weight_piece, 3, 1, wS, wR)
    get_value.wait()
    give_value.wait_recv()
    give_qk.wait_recv()
    QKf[rows(x, 4 * fd), :] = qkown[:, mine] + qkin[...]
    weight_ring.first()

    W[2 * HD + 4 * count :, :] = jnp.zeros((W.shape[0] - 2 * HD - 4 * count, Dh), bf16)
    for g in range(S // GROUP):
        VBD[g] = jnp.zeros(VBD.shape[1:], bf16)
    Sg[:, FEATURES:, :] = jnp.zeros((S, 2 * LANES - FEATURES, HD), bf16)

    out_ring = Ring("seq", S, z, lambda p, way, step, b: WO.at[slot_of(S, way, step), HD * p : HD * (p + 1)], 2, 1, oS, oR)

    def swaps(n):
        first, slots = sets[n]
        here = slice(first * R, (first + slots) * R)
        return (remote(Pn.at[here, HD : 2 * HD + LANES], Rn.at[here], e2S.at[n, 0], e2R.at[n, 0], sub=other),
                remote(PT.at[:, here], RT.at[:, here], e2S.at[n, 1], e2R.at[n, 1], sub=other))

    def project(n):
        first, slots = sets[n]
        for j in range(first, first + slots, GROUP):
            lhs = T[j : j + GROUP].reshape(GROUP * R, Dh)
            here = slice(j * R, (j + GROUP) * R)
            Pn[here, :] = nt(lhs, W[...])
            PT[:, here] = nt(W[2 * HD : 2 * HD + 4 * count, :], lhs)
        for copy in swaps(n):
            copy.start()

    def gather_piece(n):
        first, slots = sets[n]

        def piece(p, way, step, b):
            if p == 0:
                return Vp.at[b, first : first + slots]
            return Kg.at[first // GROUP : (first + slots) // GROUP, :, rows(b, LANES)]

        return piece

    gather = [Ring("fsdp", X, x, gather_piece(n), 2, 1, kS.at[n], kR.at[n]) for n in range(len(sets))]

    def combine(n):
        first, slots = sets[n]
        here = slice(first * R, (first + slots) * R)
        for copy in swaps(n):
            copy.wait_recv()
        Vp[x, first : first + slots] = (Pn[here, :HD] + Rn[here, :HD]).astype(bf16).reshape(slots, R, HD)
        entries = (PT[:, here] + RT[:, here]).astype(bf16)
        keys = mm(pickv[...], entries).astype(bf16)
        for g in range(slots // GROUP):
            Kg[first // GROUP + g, :, rows(x, LANES)] = keys[:, g * LANES : (g + 1) * LANES]
        gather[n].first()
        Qn[here, :] = (Pn[here, 2 * HD :] + Rn[here, HD:]).astype(bf16)

    row = lax.broadcasted_iota(jnp.int32, (GROUP * R, X * LANES), 0)
    key = lax.broadcasted_iota(jnp.int32, (GROUP * R, X * LANES), 1)
    seen = (key // LANES) * R + key % R <= x * R + row % R
    lane = lax.broadcasted_iota(jnp.int32, (GROUP * R, LANES), 1)

    def within(g):
        keys = Kg[g]
        feats = ((mm(ktab[0], keys) + upright[0][:, :1]) * (mm(ktab[1], keys) + upright[1][:, :1])).astype(bf16)
        for b in range(X):
            for i in range(GROUP):
                VBD[g, b * LANES + i * R : b * LANES + (i + 1) * R, i * HD : (i + 1) * HD] = Vp[b, GROUP * g + i]
        spread = VBD[g]
        contrib = mm(feats, spread)
        for i in range(GROUP):
            Cs[GROUP * g + i] = contrib[:, i * HD : (i + 1) * HD]
        entries = Qn[g * GROUP * R : (g + 1) * GROUP * R, :]
        query_feats = ((mm(entries, qtabv[0]) + bias[0:1, :]) * (mm(entries, qtabv[1]) + bias[1:2, :])).astype(bf16)
        Fq[g] = query_feats
        line = jnp.where(lane <= count, query_feats[:, :LANES], jnp.zeros((GROUP * R, LANES), bf16))
        s = mm(line, feats[:LANES])
        weight = jnp.where(seen, 0.5 * (s * s) + 0.5, 0.0).astype(bf16)
        near = mm(weight, spread)
        for i in range(GROUP):
            num[g, i * R : (i + 1) * R, :] = near[i * R : (i + 1) * R, i * HD : (i + 1) * HD]

    jobs = [(5.6 * s, 0, functools.partial(token_ring.tick, s)) for s in range(1, S // 2 + 1)]
    jobs += [(3.0 + 8.0 * s, 1, functools.partial(weight_ring.tick, s)) for s in range(1, X // 2 + 1)]
    weights_at = 3.0 + 8.0 * (X // 2)

    def keep_qk():
        W[2 * HD : 2 * HD + 4 * count, :] = QKf[...].astype(bf16)

    jobs.append((weights_at + 0.1, 2, keep_qk))

    def out_first():
        get_out.wait()
        out_ring.first()

    jobs.append((5.6 * (S // 2) - 0.5, 2, out_first))
    now = weights_at
    for n, (first, slots) in enumerate(sets):
        last = first + slots - 1
        now = max(now + 1.0, 5.6 * ((last + 1) // 2))
        jobs.append((now + 0.2, 2, functools.partial(project, n)))
        jobs.append((now + 3.0, 2, functools.partial(combine, n)))
        for step in range(1, X // 2 + 1):
            jobs.append((now + 3.0 + 2.2 * step, 2, functools.partial(gather[n].tick, step)))
        for g in range(first // GROUP, (first + slots) // GROUP):
            jobs.append((now + 4.0 + 2.2 * (X // 2) + 0.1 * g, 2, functools.partial(within, g)))
        now = now + 3.0
    jobs += [(5.6 * (S // 2 + s), 0, functools.partial(out_ring.tick, s)) for s in range(1, min(2, S // 2 - 1) + 1)]

    get_tab.wait()
    get_pick.wait()
    for _, _, job in sorted(jobs, key=lambda j: j[:2]):
        job()
    done = min(2, S // 2 - 1)

    def prefix(p, total):
        away = lax.rem(p + S - z, S)
        slot = 2 * away + (away // (S // 2)) * (2 * S - 1 - 4 * away)
        Sg[slot, :FEATURES, :] = total.astype(bf16)
        return total + Cs[slot]

    lax.fori_loop(0, S, prefix, jnp.zeros((FEATURES, HD), f32))

    for g in range(S // GROUP):
        states = jnp.concatenate([Sg[GROUP * g + i] for i in range(GROUP)], axis=1)
        far = mm(Fq[g], states)
        for i in range(GROUP):
            here = slice(i * R, (i + 1) * R)
            widened = (num[g, here, :] + far[here, i * HD : (i + 1) * HD]).astype(bf16).astype(f32)
            power = jnp.mean(widened * widened, axis=1, keepdims=True)
            A1[GROUP * g + i] = (widened * lax.rsqrt(power + 1e-06) * hgain[...]).astype(bf16)

    lanes = pl.ds(pl.multiple_of(c * HD, LANES), HD)

    def to_plane(k):
        up, down = (slot_of(S, 1, k), slot_of(S, 0, k)) if k <= S // 2 else (slot_of(S, 0, S - k), slot_of(S, 1, S - k))
        return remote(A1.at[up], Att.at[down, rows(x, R), lanes], zS.at[k], zR.at[k], seq=lax.rem(z + k, S))

    far_first = sorted(range(1, S), key=lambda k: -min(k, S - k))
    for k in far_first:
        to_plane(k).start()
    Att[0, rows(x, R), lanes] = A1[0]

    upper = S // 2

    def share(p, way, step, b):
        return Att.at[upper * p : upper * (p + 1), rows(b, R), lanes]

    def relay(way, step, p, b):
        ref = share(p, way, step, b)
        return remote(ref, ref, relS.at[way, step - 1, p], relR.at[way, step - 1, p], sub=other)

    def own_relay(p):
        ref = share(p, 0, 0, x)
        return remote(ref, ref, ownS.at[p], ownR.at[p], sub=other)

    share_ring = Ring("fsdp", X, x, share, 2, 1, aS, aR)

    def arrive(p):
        for k in far_first:
            down = slot_of(S, 0, k) if k <= S // 2 else slot_of(S, 1, S - k)
            if down // upper == p:
                to_plane(k).wait_recv()
        share_ring.first([p])
        own_relay(p).start()

    def service():
        nonlocal done
        if done < S // 2 - 1:
            done += 1
            out_ring.tick(done)

    service()
    arrive(0)
    arrive(1)
    service()
    for step in range(1, X // 2 + 1):
        share_ring.tick(step, lambda way, s, p, b: relay(way, s, p, b).start())
        if step % 2 == 1:
            service()

    for p in range(2):
        own_relay(p).wait_recv()
    for step in range(1, X // 2 + 1):
        for p in range(2):
            for way in range(2):
                if share_ring.moves(way, step, p):
                    relay(way, step, p, share_ring.block(way, step)).wait_recv()

    acc[...] = mm(Att[0], WO[0])

    def add(j):
        acc[...] += mm(Att[j], WO[j])

    @pl.loop(1, 2 * done + 1)
    def _(j):
        add(j)

    while done < S // 2 - 1:
        service()
        add(2 * done - 1)
        add(2 * done)
    out_ring.tick(S // 2)
    out[...] = (acc[...] + mm(Att[S - 1], WO[S - 1])).astype(bf16)

    token_ring.drain()
    weight_ring.drain()
    out_ring.drain()
    share_ring.drain()
    for ring in gather:
        ring.drain()
    give_value.wait_send()
    give_qk.wait_send()
    for n in range(len(sets)):
        for copy in swaps(n):
            copy.wait_send()
    for k in range(1, S):
        to_plane(k).wait_send()
    for p in range(2):
        own_relay(p).wait_send()
    for step in range(1, X // 2 + 1):
        for p in range(2):
            for way in range(2):
                if share_ring.moves(way, step, p):
                    relay(way, step, p, x).wait_send()


def solution(mesh):
    S, X = mesh.shape["seq"], mesh.shape["fsdp"]
    if S >= 16:
        sets = [(0, S // 2)] + [(first, GROUP) for first in range(S // 2, S, GROUP)]
    else:
        sets = [(first, GROUP) for first in range(0, S, GROUP)]

    def per_device(tokens, norm_gain, w_query, w_key, w_value, head_gain, w_out):
        Ppl, D = tokens.shape
        fd, vd = w_query.shape[1], w_value.shape[1]
        HD, R, Dh, C = X * vd, Ppl // X, D // 2, w_out.shape[2]
        count, groups = X * fd, S // GROUP
        qtab, pick, ktab, bias, upright = feature_tables(X, fd)
        any_ref = pl.BlockSpec(memory_space=pl.ANY)
        vm = pl.BlockSpec(memory_space=pltpu.VMEM)
        dma = pltpu.SemaphoreType.DMA
        V = pltpu.VMEM
        scratch = [
            V((R, D), bf16),
            V((S, R, Dh), bf16),
            V((2 * HD + LANES, Dh), bf16),
            V((4 * count, Dh), f32),
            V((4 * fd, D), f32),
            V((4 * fd, Dh), f32),
            V((S * R, 2 * HD + LANES), f32),
            V((S * R, HD + LANES), f32),
            V((4 * count, S * R), f32),
            V((4 * count, S * R), f32),
            V((S * R, LANES), bf16),
            V((X, S, R, HD), bf16),
            V((groups, count, X * LANES), bf16),
            V((groups, X * LANES, GROUP * HD), bf16),
            V((S, FEATURES, HD), f32),
            V((S, 2 * LANES, HD), bf16),
            V((groups, GROUP * R, 2 * LANES), bf16),
            V((groups, GROUP * R, HD), f32),
            V((S, R, HD), bf16),
            V((S, Ppl, 2 * HD), bf16),
            V((S, 2 * HD, C), bf16),
            V((Ppl, C), f32),
            V((2, LANES, 2 * LANES), bf16),
            V((count, 4 * count), bf16),
            dma((5,)),
            dma((2, S // 2, 2)), dma((2, S // 2, 2)),
            dma((2, X // 2, 3)), dma((2, X // 2, 3)),
            dma((2, S // 2, 2)), dma((2, S // 2, 2)),
            dma((2, X // 2, 2)), dma((2, X // 2, 2)),
            dma((len(sets), 2, X // 2, 2)), dma((len(sets), 2, X // 2, 2)),
            dma((2,)), dma((2,)),
            dma((len(sets), 2)), dma((len(sets), 2)),
            dma((S,)), dma((S,)),
            dma((2,)), dma((2,)),
            dma((2, X // 2, 2)), dma((2, X // 2, 2)),
        ]
        return pl.pallas_call(
            functools.partial(layer, S, X, sets),
            out_shape=jax.ShapeDtypeStruct((Ppl, C), bf16),
            in_specs=[any_ref, vm, vm, vm, any_ref, vm, any_ref, any_ref, any_ref, vm, vm, vm],
            out_specs=vm,
            scratch_shapes=scratch,
            compiler_params=pltpu.CompilerParams(
                collective_id=0, has_side_effects=True, vmem_limit_bytes=67043328),
            name="layer",
        )(
            tokens,
            norm_gain.reshape(1, D),
            w_query.reshape(fd, D),
            w_key.reshape(fd, D),
            w_value.reshape(vd, D),
            head_gain.reshape(1, HD),
            w_out.reshape(2 * HD, C),
            qtab,
            pick,
            ktab,
            bias,
            upright,
        )

    in_specs = (
        P(("groups", "seq"), None),
        P(),
        P(("seq", "sub"), "fsdp", None),
        P(("seq", "sub"), "fsdp", None),
        P(("seq", "sub"), "fsdp", None),
        P(),
        P("seq", None, ("fsdp", "sub")),
    )
    out_specs = P(("groups", "seq"), ("fsdp", "sub"))
    return jax.shard_map(
        per_device, mesh=mesh, in_specs=in_specs, out_specs=out_specs, check_vma=False
    )
```

time: 189 us -> 165 us (0.87)
  Pallas kernels: 179 us -> 163 us
  local copies, waits for them, and re-layouts: 9.46 us -> 1.67 us
    pallas_call x1, Pallas kernels: 179 us -> 163 us  [per_device(): pl.pallas_call(functools.partial(layer, S, X, sets), out_shape=jax.ShapeD...]
    unnamed x19 -> x1, local copies, waits for them, and re-layouts: 9.46 us -> 1.67 us
where the time goes in v2:
time: 165 us
  Pallas kernels  163 us (99%)
  local copies, waits for them, and re-layouts  1.67 us (1%)
    pallas_call x1, Pallas kernels, per_device(): pl.pallas_call(functools.partial(layer, S, X, sets), out_shape=jax.ShapeD...  163 us

profile of v2, /device:TPU:65, one launch (start us, length us, event | category | flops | bytes accessed | tf_op | source)
XLA Modules:
  0.0 164.7 jit_solution(17172133619216061810)
XLA Ops:
  0.0 163.1 %layer.1 = bf16[256,512]{1,0:T(8,128)(2,1)} custom-call(bf16[256,8192]{1,0:T(8,128)(2,1)} %tokens.1, f32[1,8192]{1,0:T(1,128)} %bitcast.8, bf16[2,8192]{1,0:T(2,128)(2,1)} %bitcast.9, bf16[2,8192]{1,0:T(2,128)(2,1)} %bitcast.10, bf16[16,8192]{1,0:T(8,128)(2,1)} %bitcast.6, f32[1,128]{1,0:T(1,128)} %bitcast.11, bf16[256,512]{1,0:T(8,128)(2,1)} %bitcast.7, ...), custom_call_target="tpu_custom_call" | custom-call | tf_op jit(solution)/shard_map/layer/pallas_call | solution.py:474
  163.1 1.7 %copy.14 = bf16[256,512]{1,0:T(8,128)(2,1)} copy(bf16[256,512]{1,0:T(8,128)(2,1)} %layer.1) | data formatting | bytes 524288

commit v3 on v2

--- a/solution.py
+++ b/solution.py
@@ -80,16 +80,15 @@
             for way in range(2):
                 self.start(way, 1, p)
 
-    def tick(self, step, arrived=None):
-        for p in range(self.pieces):
-            for way in range(2):
-                if self.moves(way, step, p):
-                    block = self.block(way, step)
-                    ref = self.piece(p, way, step, block)
-                    self.copy(way, step, p, ref, ref).wait_recv()
-                    self.start(way, step + 1, p)
-                    if arrived is not None:
-                        arrived(way, step, p, block)
+    def tick(self, step, p, arrived=None):
+        for way in range(2):
+            if self.moves(way, step, p):
+                block = self.block(way, step)
+                ref = self.piece(p, way, step, block)
+                self.copy(way, step, p, ref, ref).wait_recv()
+                self.start(way, step + 1, p)
+                if arrived is not None:
+                    arrived(way, step, p, block)
 
     def drain(self):
         for step in range(1, self.last + 1):
@@ -114,9 +113,9 @@
     return size - 1 if step == size // 2 else 2 * step - 1 + way
 
 
-def layer(S, X, sets, tokens, gain, wq, wk, wv, hgain, wo, qtab, pick, ktab, bias, upright, out,
-          tokv, T, W, QKf, qkown, qkin, Pn, Rn, PT, RT, Qn, Vp, Kg, VBD, Cs, Sg, Fq, num, A1, Att, WO, acc, qtabv, pickv,
-          lsem, tS, tR, wS, wR, oS, oR, aS, aR, kS, kR, pS, pR, e2S, e2R, zS, zR, ownS, ownR, relS, relR):
+def layer(S, X, sets, tokens, gain_hbm, wq_hbm, wk_hbm, wv, hgain_hbm, wo, qtab, pick, ktab_hbm, bias_hbm, upright_hbm, out,
+          gain, wq, wk, hgain, ktab, bias, upright, tokv, T, W, QKf, QKb, qkown, qkin, Pn, Rn, PT, RT, Qn, Vp, Kg, VBD, Cs, Sg, Fq, num, A1, Att, WO, acc, qtabv, pickv,
+          lsem, tS, tR, wS, wR, oS, oR, aS, aR, kS, kR, dS, dR, pS, pR, e2S, e2R, zS, zR, ownS, ownR, relS, relR):
     x, z, c = lax.axis_index("fsdp"), lax.axis_index("seq"), lax.axis_index("sub")
     R, D = tokv.shape
     Dh = D // 2
@@ -145,12 +144,40 @@
     get_out = pltpu.make_async_copy(wo, WO.at[0], lsem.at[2])
     get_tab = pltpu.make_async_copy(qtab.at[c], qtabv, lsem.at[3])
     get_pick = pltpu.make_async_copy(pick.at[c], pickv, lsem.at[4])
-    get_tokens.start()
-    get_value.start()
-    get_out.start()
-    get_tab.start()
-    get_pick.start()
-
+    small = [(gain_hbm, gain), (wq_hbm, wq), (wk_hbm, wk), (hgain_hbm, hgain), (ktab_hbm, ktab), (bias_hbm, bias), (upright_hbm, upright)]
+    get_gain, get_wq, get_wk, *get_later = [
+        pltpu.make_async_copy(src, dst, lsem.at[5 + i]) for i, (src, dst) in enumerate(small)]
+    get_later += [get_tab, get_pick]
+    for copy in [get_tokens, get_gain, get_wq, get_wk, get_value, get_out] + get_later:
+        copy.start()
+
+    get_tokens.wait()
+    chunk = min(1024, D)
+
+    def squares(i, total):
+        part = tokv[:, pl.ds(pl.multiple_of(i * chunk, chunk), chunk)].astype(f32)
+        return total + jnp.sum(part * part, axis=1, keepdims=True)
+
+    meansq = lax.fori_loop(0, D // chunk, squares, jnp.zeros((R, 1), f32)) / D
+    scale = lax.rsqrt(meansq + 1e-05)
+    chunk = min(1024, Dh)
+
+    get_gain.wait()
+
+    @pl.loop(0, Dh // chunk)
+    def _(i):
+        here = pl.ds(pl.multiple_of(c * Dh + i * chunk, chunk), chunk)
+        part = tokv[:, here].astype(f32) * scale * gain[:, here]
+        T[0, :, pl.ds(pl.multiple_of(i * chunk, chunk), chunk)] = part.astype(bf16)
+
+    pl.semaphore_wait(barrier, len(greeted))
+
+    half = R // 2
+    token_ring = Ring("seq", S, z, lambda p, way, step, b: T.at[slot_of(S, way, step), half * p : half * (p + 1)], 2, 1, tS, tR)
+    token_ring.first()
+
+    get_wq.wait()
+    get_wk.wait()
     qkown[...] = jnp.zeros_like(qkown)
     for head in range(2):
         @pl.when(c == head)
@@ -159,29 +186,6 @@
             qkown[base : base + fd, :] = wq[...].astype(f32)
             qkown[base + fd : base + 2 * fd, :] = wk[...].astype(f32)
 
-    get_tokens.wait()
-    chunk = min(1024, D)
-
-    def squares(i, total):
-        part = tokv[:, pl.ds(pl.multiple_of(i * chunk, chunk), chunk)].astype(f32)
-        return total + jnp.sum(part * part, axis=1, keepdims=True)
-
-    meansq = lax.fori_loop(0, D // chunk, squares, jnp.zeros((R, 1), f32)) / D
-    scale = lax.rsqrt(meansq + 1e-05)
-    chunk = min(1024, Dh)
-
-    @pl.loop(0, Dh // chunk)
-    def _(i):
-        here = pl.ds(pl.multiple_of(c * Dh + i * chunk, chunk), chunk)
-        part = tokv[:, here].astype(f32) * scale * gain[:, here]
-        T[0, :, pl.ds(pl.multiple_of(i * chunk, chunk), chunk)] = part.astype(bf16)
-
-    pl.semaphore_wait(barrier, len(greeted))
-
-    half = R // 2
-    token_ring = Ring("seq", S, z, lambda p, way, step, b: T.at[slot_of(S, way, step), half * p : half * (p + 1)], 2, 1, tS, tR)
-    token_ring.first()
-
     give_value = remote(wv.at[:, theirs], W.at[pl.ds(pl.multiple_of(HD + x * vd, vd), vd)], pS.at[0], pR.at[0], sub=other)
     give_qk = remote(qkown.at[:, theirs], qkin, pS.at[1], pR.at[1], sub=other)
     give_value.start()
@@ -189,14 +193,14 @@
 
     def weight_piece(p, way, step, b):
         if p == 2:
-            return QKf.at[rows(b, 4 * fd)]
+            return QKb.at[b]
         return W.at[pl.ds(pl.multiple_of(HD * p + b * vd, vd), vd)]
 
     weight_ring = Ring("fsdp", X, x, weight_piece, 3, 1, wS, wR)
     get_value.wait()
     give_value.wait_recv()
     give_qk.wait_recv()
-    QKf[rows(x, 4 * fd), :] = qkown[:, mine] + qkin[...]
+    QKb[x] = (qkown[:, mine] + qkin[...]).astype(bf16)
     weight_ring.first()
 
     W[2 * HD + 4 * count :, :] = jnp.zeros((W.shape[0] - 2 * HD - 4 * count, Dh), bf16)
@@ -232,7 +236,12 @@
 
         return piece
 
-    gather = [Ring("fsdp", X, x, gather_piece(n), 2, 1, kS.at[n], kR.at[n]) for n in range(len(sets))]
+    gather = Ring("fsdp", X, x, gather_piece(0), 2, 1, kS, kR)
+    nearest_last = sorted(range(1, X), key=lambda k: -min(k, X - k))
+
+    def direct(n, k, p, owner):
+        ref = gather_piece(n)(p, 0, 0, owner)
+        return remote(ref, ref, dS.at[n, k, p], dR.at[n, k, p], fsdp=lax.rem(x + k, X))
 
     def combine(n):
         first, slots = sets[n]
@@ -244,7 +253,12 @@
         keys = mm(pickv[...], entries).astype(bf16)
         for g in range(slots // GROUP):
             Kg[first // GROUP + g, :, rows(x, LANES)] = keys[:, g * LANES : (g + 1) * LANES]
-        gather[n].first()
+        if n == 0:
+            gather.first()
+        else:
+            for k in nearest_last:
+                for p in range(2):
+                    direct(n, k, p, x).start()
         Qn[here, :] = (Pn[here, 2 * HD :] + Rn[here, HD:]).astype(bf16)
 
     row = lax.broadcasted_iota(jnp.int32, (GROUP * R, X * LANES), 0)
@@ -272,38 +286,19 @@
         for i in range(GROUP):
             num[g, i * R : (i + 1) * R, :] = near[i * R : (i + 1) * R, i * HD : (i + 1) * HD]
 
-    jobs = [(5.6 * s, 0, functools.partial(token_ring.tick, s)) for s in range(1, S // 2 + 1)]
-    jobs += [(3.0 + 8.0 * s, 1, functools.partial(weight_ring.tick, s)) for s in range(1, X // 2 + 1)]
-    weights_at = 3.0 + 8.0 * (X // 2)
-
     def keep_qk():
+        for b in range(X):
+            QKf[4 * fd * b : 4 * fd * (b + 1), :] = QKb[b].astype(f32)
         W[2 * HD : 2 * HD + 4 * count, :] = QKf[...].astype(bf16)
-
-    jobs.append((weights_at + 0.1, 2, keep_qk))
 
     def out_first():
         get_out.wait()
         out_ring.first()
 
-    jobs.append((5.6 * (S // 2) - 0.5, 2, out_first))
-    now = weights_at
-    for n, (first, slots) in enumerate(sets):
-        last = first + slots - 1
-        now = max(now + 1.0, 5.6 * ((last + 1) // 2))
-        jobs.append((now + 0.2, 2, functools.partial(project, n)))
-        jobs.append((now + 3.0, 2, functools.partial(combine, n)))
-        for step in range(1, X // 2 + 1):
-            jobs.append((now + 3.0 + 2.2 * step, 2, functools.partial(gather[n].tick, step)))
-        for g in range(first // GROUP, (first + slots) // GROUP):
-            jobs.append((now + 4.0 + 2.2 * (X // 2) + 0.1 * g, 2, functools.partial(within, g)))
-        now = now + 3.0
-    jobs += [(5.6 * (S // 2 + s), 0, functools.partial(out_ring.tick, s)) for s in range(1, min(2, S // 2 - 1) + 1)]
-
-    get_tab.wait()
-    get_pick.wait()
-    for _, _, job in sorted(jobs, key=lambda j: j[:2]):
-        job()
-    done = min(2, S // 2 - 1)
+    def landed(n):
+        for k in nearest_last:
+            for p in range(2):
+                direct(n, k, p, lax.rem(x + X - k, X)).wait_recv()
 
     def prefix(p, total):
         away = lax.rem(p + S - z, S)
@@ -311,17 +306,6 @@
         Sg[slot, :FEATURES, :] = total.astype(bf16)
         return total + Cs[slot]
 
-    lax.fori_loop(0, S, prefix, jnp.zeros((FEATURES, HD), f32))
-
-    for g in range(S // GROUP):
-        states = jnp.concatenate([Sg[GROUP * g + i] for i in range(GROUP)], axis=1)
-        far = mm(Fq[g], states)
-        for i in range(GROUP):
-            here = slice(i * R, (i + 1) * R)
-            widened = (num[g, here, :] + far[here, i * HD : (i + 1) * HD]).astype(bf16).astype(f32)
-            power = jnp.mean(widened * widened, axis=1, keepdims=True)
-            A1[GROUP * g + i] = (widened * lax.rsqrt(power + 1e-06) * hgain[...]).astype(bf16)
-
     lanes = pl.ds(pl.multiple_of(c * HD, LANES), HD)
 
     def to_plane(k):
@@ -329,14 +313,25 @@
         return remote(A1.at[up], Att.at[down, rows(x, R), lanes], zS.at[k], zR.at[k], seq=lax.rem(z + k, S))
 
     far_first = sorted(range(1, S), key=lambda k: -min(k, S - k))
-    for k in far_first:
-        to_plane(k).start()
-    Att[0, rows(x, R), lanes] = A1[0]
-
-    upper = S // 2
+
+    def attend():
+        lax.fori_loop(0, S, prefix, jnp.zeros((FEATURES, HD), f32))
+        for g in range(S // GROUP):
+            states = jnp.concatenate([Sg[GROUP * g + i] for i in range(GROUP)], axis=1)
+            far = mm(Fq[g], states)
+            for i in range(GROUP):
+                here = slice(i * R, (i + 1) * R)
+                widened = (num[g, here, :] + far[here, i * HD : (i + 1) * HD]).astype(bf16).astype(f32)
+                power = jnp.mean(widened * widened, axis=1, keepdims=True)
+                A1[GROUP * g + i] = (widened * lax.rsqrt(power + 1e-06) * hgain[...]).astype(bf16)
+        for k in far_first:
+            to_plane(k).start()
+        Att[0, rows(x, R), lanes] = A1[0]
+
+    quarter = S // GROUP
 
     def share(p, way, step, b):
-        return Att.at[upper * p : upper * (p + 1), rows(b, R), lanes]
+        return Att.at[GROUP * p : GROUP * (p + 1), rows(b, R), lanes]
 
     def relay(way, step, p, b):
         ref = share(p, way, step, b)
@@ -346,61 +341,97 @@
         ref = share(p, 0, 0, x)
         return remote(ref, ref, ownS.at[p], ownR.at[p], sub=other)
 
-    share_ring = Ring("fsdp", X, x, share, 2, 1, aS, aR)
+    share_ring = Ring("fsdp", X, x, share, quarter, quarter // 2, aS, aR)
 
     def arrive(p):
         for k in far_first:
             down = slot_of(S, 0, k) if k <= S // 2 else slot_of(S, 1, S - k)
-            if down // upper == p:
+            if down // GROUP == p:
                 to_plane(k).wait_recv()
         share_ring.first([p])
         own_relay(p).start()
 
-    def service():
-        nonlocal done
-        if done < S // 2 - 1:
-            done += 1
-            out_ring.tick(done)
-
-    service()
-    arrive(0)
-    arrive(1)
-    service()
-    for step in range(1, X // 2 + 1):
-        share_ring.tick(step, lambda way, s, p, b: relay(way, s, p, b).start())
-        if step % 2 == 1:
-            service()
-
-    for p in range(2):
+    def spread(step, p):
+        share_ring.tick(step, p, lambda way, s, p, b: relay(way, s, p, b).start())
+
+    def whole(p):
         own_relay(p).wait_recv()
-    for step in range(1, X // 2 + 1):
-        for p in range(2):
+        for step in range(1, X // 2 + 1):
             for way in range(2):
                 if share_ring.moves(way, step, p):
                     relay(way, step, p, share_ring.block(way, step)).wait_recv()
 
-    acc[...] = mm(Att[0], WO[0])
-
-    def add(j):
-        acc[...] += mm(Att[j], WO[j])
-
-    @pl.loop(1, 2 * done + 1)
-    def _(j):
-        add(j)
-
-    while done < S // 2 - 1:
-        service()
-        add(2 * done - 1)
-        add(2 * done)
-    out_ring.tick(S // 2)
-    out[...] = (acc[...] + mm(Att[S - 1], WO[S - 1])).astype(bf16)
+    def product(first, last):
+        lhs = jnp.concatenate([Att[j] for j in range(first, last)], axis=1)
+        term = mm(lhs, WO[first:last].reshape((last - first) * 2 * HD, WO.shape[2]))
+        if last == S:
+            out[...] = (acc[...] + term).astype(bf16)
+        else:
+            acc[...] = term if first == 0 else acc[...] + term
+
+    jobs = []
+
+    def at(time, job, *details):
+        jobs.append((time, len(jobs), functools.partial(job, *details)))
+
+    half_z, half_x = S // 2, X // 2
+    for step in range(1, half_z + 1):
+        for p in range(2):
+            at(9.5 + 5.9 * (step - 1) + 2.95 * (p + 1), token_ring.tick, step, p)
+    for step in range(1, half_x + 1):
+        for p in range(3):
+            at(9.5 + 7.2 * (step - 1) + 2.4 * (p + 1), weight_ring.tick, step, p)
+    held = 9.6 + 7.2 * half_x
+    turn = 9.5 + 5.9 * half_z
+    at(turn - 5.8, out_first)
+    at(held, keep_qk)
+    free = held
+    for n, (first, slots) in enumerate(sets):
+        last = 9.6 + 5.9 * ((first + slots) // 2)
+        start = max(free, last)
+        at(start, project, n)
+        at(start + 4.0, combine, n)
+        if n == 0:
+            for step in range(1, half_x + 1):
+                for p in range(2):
+                    at(start + 4.0 + 3.2 * (step - 1) + 1.6 * (p + 1), gather.tick, step, p)
+            end = start + 4.2 + 3.2 * half_x
+        else:
+            end = start + 12.5
+            at(end, landed, n)
+        for g in range(first // GROUP, (first + slots) // GROUP):
+            at(end + 0.1, within, g)
+        free = start + 4.1
+    at(end + 1.0, attend)
+    for p in range(quarter):
+        at(end + 9.0 + 0.7 * p, arrive, p)
+    for step in range(1, half_x + 1):
+        for p in range(quarter):
+            at(end + 11.0 + 3.2 * (step - 1) + 0.8 * (p + 1), spread, step, p)
+    for p in range(quarter):
+        time = end + 12.0 + 3.2 * half_x + 0.5 * p
+        at(time, whole, p)
+        ready = turn + 5.7 * min(2 * p + 2, half_z - 1) + 0.1
+        at(max(time, ready), product, GROUP * p, min(GROUP * (p + 1), S - 1))
+    at(max(time, turn + 5.7 * half_z) + 0.2, product, S - 1, S)
+    for step in range(1, half_z + 1):
+        for p in range(2):
+            at(turn + 5.7 * (step - 1) + 2.85 * (p + 1), out_ring.tick, step, p)
+
+    for copy in get_later:
+        copy.wait()
+    for _, _, job in sorted(jobs, key=lambda job: job[:2]):
+        job()
 
     token_ring.drain()
     weight_ring.drain()
     out_ring.drain()
     share_ring.drain()
-    for ring in gather:
-        ring.drain()
+    gather.drain()
+    for n in range(1, len(sets)):
+        for k in range(1, X):
+            for p in range(2):
+                direct(n, k, p, x).wait_send()
     give_value.wait_send()
     give_qk.wait_send()
     for n in range(len(sets)):
@@ -408,10 +439,10 @@
             copy.wait_send()
     for k in range(1, S):
         to_plane(k).wait_send()
-    for p in range(2):
+    for p in range(quarter):
         own_relay(p).wait_send()
     for step in range(1, X // 2 + 1):
-        for p in range(2):
+        for p in range(quarter):
             for way in range(2):
                 if share_ring.moves(way, step, p):
                     relay(way, step, p, x).wait_send()
@@ -419,10 +450,8 @@
 
 def solution(mesh):
     S, X = mesh.shape["seq"], mesh.shape["fsdp"]
-    if S >= 16:
-        sets = [(0, S // 2)] + [(first, GROUP) for first in range(S // 2, S, GROUP)]
-    else:
-        sets = [(first, GROUP) for first in range(0, S, GROUP)]
+    early = max(S // 2, GROUP)
+    sets = [(0, early)] + [(first, GROUP) for first in range(early, S, GROUP)]
 
     def per_device(tokens, norm_gain, w_query, w_key, w_value, head_gain, w_out):
         Ppl, D = tokens.shape
@@ -430,15 +459,23 @@
         HD, R, Dh, C = X * vd, Ppl // X, D // 2, w_out.shape[2]
         count, groups = X * fd, S // GROUP
         qtab, pick, ktab, bias, upright = feature_tables(X, fd)
-        any_ref = pl.BlockSpec(memory_space=pl.ANY)
+        in_hbm = pl.BlockSpec(memory_space=pltpu.MemorySpace.HBM)
         vm = pl.BlockSpec(memory_space=pltpu.VMEM)
         dma = pltpu.SemaphoreType.DMA
         V = pltpu.VMEM
         scratch = [
+            V((1, D), f32),
+            V((fd, D), bf16),
+            V((fd, D), bf16),
+            V((1, HD), f32),
+            V((2, FEATURES, count), bf16),
+            V((8, 2 * LANES), f32),
+            V((2, FEATURES, LANES), f32),
             V((R, D), bf16),
             V((S, R, Dh), bf16),
             V((2 * HD + LANES, Dh), bf16),
             V((4 * count, Dh), f32),
+            V((X, 4 * fd, Dh), bf16),
             V((4 * fd, D), f32),
             V((4 * fd, Dh), f32),
             V((S * R, 2 * HD + LANES), f32),
@@ -459,26 +496,27 @@
             V((Ppl, C), f32),
             V((2, LANES, 2 * LANES), bf16),
             V((count, 4 * count), bf16),
-            dma((5,)),
+            dma((12,)),
             dma((2, S // 2, 2)), dma((2, S // 2, 2)),
             dma((2, X // 2, 3)), dma((2, X // 2, 3)),
             dma((2, S // 2, 2)), dma((2, S // 2, 2)),
+            dma((2, X // 2, groups)), dma((2, X // 2, groups)),
             dma((2, X // 2, 2)), dma((2, X // 2, 2)),
-            dma((len(sets), 2, X // 2, 2)), dma((len(sets), 2, X // 2, 2)),
+            dma((len(sets), X, 2)), dma((len(sets), X, 2)),
             dma((2,)), dma((2,)),
             dma((len(sets), 2)), dma((len(sets), 2)),
             dma((S,)), dma((S,)),
-            dma((2,)), dma((2,)),
-            dma((2, X // 2, 2)), dma((2, X // 2, 2)),
+            dma((groups,)), dma((groups,)),
+            dma((2, X // 2, groups)), dma((2, X // 2, groups)),
         ]
         return pl.pallas_call(
             functools.partial(layer, S, X, sets),
             out_shape=jax.ShapeDtypeStruct((Ppl, C), bf16),
-            in_specs=[any_ref, vm, vm, vm, any_ref, vm, any_ref, any_ref, any_ref, vm, vm, vm],
+            in_specs=[in_hbm] * 12,
             out_specs=vm,
             scratch_shapes=scratch,
             compiler_params=pltpu.CompilerParams(
-                collective_id=0, has_side_effects=True, vmem_limit_bytes=67043328),
+                collective_id=0, has_side_effects=True, vmem_limit_bytes=56 * 1024 * 1024),
             name="layer",
         )(
             tokens,

time: 165 us -> 156 us (0.945)
  Pallas kernels: 163 us -> 152 us
    pallas_call x1, Pallas kernels: 163 us -> 152 us  [per_device(): pl.pallas_call(functools.partial(layer, S, X, sets), out_shape=jax.ShapeD...]
where the time goes in v3:
time: 156 us; the launch traced here: 154 us
  Pallas kernels  152 us (97%)
  local copies, waits for them, and re-layouts  1.67 us (1%)
    pallas_call x1, Pallas kernels, per_device(): pl.pallas_call(functools.partial(layer, S, X, sets), out_shape=jax.ShapeD...  152 us

profile of v3, /device:TPU:65, one launch (start us, length us, event | category | flops | bytes accessed | tf_op | source)
XLA Modules:
  0.0 154.1 jit_solution(6505254264098785531)
XLA Ops:
  0.0 152.4 %layer.1 = bf16[256,512]{1,0:T(8,128)(2,1)} custom-call(bf16[256,8192]{1,0:T(8,128)(2,1)} %tokens.1, f32[1,8192]{1,0:T(1,128)} %bitcast.8, bf16[2,8192]{1,0:T(2,128)(2,1)} %bitcast.9, bf16[2,8192]{1,0:T(2,128)(2,1)} %bitcast.10, bf16[16,8192]{1,0:T(8,128)(2,1)} %bitcast.6, f32[1,128]{1,0:T(1,128)} %bitcast.11, bf16[256,512]{1,0:T(8,128)(2,1)} %bitcast.7, ...), custom_call_target="tpu_custom_call" | custom-call | tf_op jit(solution)/shard_map/layer/pallas_call | solution.py:512
  152.4 1.7 %copy.14 = bf16[256,512]{1,0:T(8,128)(2,1)} copy(bf16[256,512]{1,0:T(8,128)(2,1)} %layer.1) | data formatting | bytes 524288

commit v4 on v3

--- a/solution.py
+++ b/solution.py
@@ -139,7 +139,12 @@
     for device in greeted:
         pl.semaphore_signal(barrier, inc=1, device_id=device, device_id_type=MESH)
 
-    get_tokens = pltpu.make_async_copy(tokens.at[rows(x, R)], tokv, lsem.at[0])
+    half = R // 2
+    get_tokens = [
+        pltpu.make_async_copy(
+            tokens.at[pl.ds(pl.multiple_of(x * R + half * p, half), half)], tokv.at[half * p : half * (p + 1)], lsem.at[12 + p])
+        for p in range(2)
+    ]
     get_value = pltpu.make_async_copy(wv.at[:, mine], W.at[rows(x, vd)], lsem.at[1])
     get_out = pltpu.make_async_copy(wo, WO.at[0], lsem.at[2])
     get_tab = pltpu.make_async_copy(qtab.at[c], qtabv, lsem.at[3])
@@ -148,33 +153,8 @@
     get_gain, get_wq, get_wk, *get_later = [
         pltpu.make_async_copy(src, dst, lsem.at[5 + i]) for i, (src, dst) in enumerate(small)]
     get_later += [get_tab, get_pick]
-    for copy in [get_tokens, get_gain, get_wq, get_wk, get_value, get_out] + get_later:
+    for copy in get_tokens + [get_gain, get_wq, get_wk, get_value, get_out] + get_later:
         copy.start()
-
-    get_tokens.wait()
-    chunk = min(1024, D)
-
-    def squares(i, total):
-        part = tokv[:, pl.ds(pl.multiple_of(i * chunk, chunk), chunk)].astype(f32)
-        return total + jnp.sum(part * part, axis=1, keepdims=True)
-
-    meansq = lax.fori_loop(0, D // chunk, squares, jnp.zeros((R, 1), f32)) / D
-    scale = lax.rsqrt(meansq + 1e-05)
-    chunk = min(1024, Dh)
-
-    get_gain.wait()
-
-    @pl.loop(0, Dh // chunk)
-    def _(i):
-        here = pl.ds(pl.multiple_of(c * Dh + i * chunk, chunk), chunk)
-        part = tokv[:, here].astype(f32) * scale * gain[:, here]
-        T[0, :, pl.ds(pl.multiple_of(i * chunk, chunk), chunk)] = part.astype(bf16)
-
-    pl.semaphore_wait(barrier, len(greeted))
-
-    half = R // 2
-    token_ring = Ring("seq", S, z, lambda p, way, step, b: T.at[slot_of(S, way, step), half * p : half * (p + 1)], 2, 1, tS, tR)
-    token_ring.first()
 
     get_wq.wait()
     get_wk.wait()
@@ -186,10 +166,37 @@
             qkown[base : base + fd, :] = wq[...].astype(f32)
             qkown[base + fd : base + 2 * fd, :] = wk[...].astype(f32)
 
+    pl.semaphore_wait(barrier, len(greeted))
     give_value = remote(wv.at[:, theirs], W.at[pl.ds(pl.multiple_of(HD + x * vd, vd), vd)], pS.at[0], pR.at[0], sub=other)
     give_qk = remote(qkown.at[:, theirs], qkin, pS.at[1], pR.at[1], sub=other)
     give_value.start()
     give_qk.start()
+
+    def token_piece(p, way, step, b):
+        up, side = divmod(p, 2)
+        return T.at[slot_of(S, way, step), half * up : half * (up + 1), Dh // 2 * side : Dh // 2 * (side + 1)]
+
+    token_ring = Ring("seq", S, z, token_piece, 4, 2, tS, tR)
+    chunk, piece = min(1024, D), min(1024, Dh)
+    get_gain.wait()
+    for p in range(2):
+        part = slice(half * p, half * (p + 1))
+        get_tokens[p].wait()
+
+        def squares(i, total):
+            values = tokv[part, pl.ds(pl.multiple_of(i * chunk, chunk), chunk)].astype(f32)
+            return total + jnp.sum(values * values, axis=1, keepdims=True)
+
+        meansq = lax.fori_loop(0, D // chunk, squares, jnp.zeros((half, 1), f32)) / D
+        scale = lax.rsqrt(meansq + 1e-05)
+
+        @pl.loop(0, Dh // piece)
+        def _(i):
+            here = pl.ds(pl.multiple_of(c * Dh + i * piece, piece), piece)
+            values = tokv[part, here].astype(f32) * scale * gain[:, here]
+            T[0, part, pl.ds(pl.multiple_of(i * piece, piece), piece)] = values.astype(bf16)
+
+        token_ring.first([2 * p, 2 * p + 1])
 
     def weight_piece(p, way, step, b):
         if p == 2:
@@ -208,7 +215,7 @@
         VBD[g] = jnp.zeros(VBD.shape[1:], bf16)
     Sg[:, FEATURES:, :] = jnp.zeros((S, 2 * LANES - FEATURES, HD), bf16)
 
-    out_ring = Ring("seq", S, z, lambda p, way, step, b: WO.at[slot_of(S, way, step), HD * p : HD * (p + 1)], 2, 1, oS, oR)
+    out_ring = Ring("seq", S, z, lambda p, way, step, b: WO.at[slot_of(S, way, step), HD // 2 * p : HD // 2 * (p + 1)], 4, 2, oS, oR)
 
     def swaps(n):
         first, slots = sets[n]
@@ -216,15 +223,15 @@
         return (remote(Pn.at[here, HD : 2 * HD + LANES], Rn.at[here], e2S.at[n, 0], e2R.at[n, 0], sub=other),
                 remote(PT.at[:, here], RT.at[:, here], e2S.at[n, 1], e2R.at[n, 1], sub=other))
 
-    def project(n):
+    def project(n, j):
         first, slots = sets[n]
-        for j in range(first, first + slots, GROUP):
-            lhs = T[j : j + GROUP].reshape(GROUP * R, Dh)
-            here = slice(j * R, (j + GROUP) * R)
-            Pn[here, :] = nt(lhs, W[...])
-            PT[:, here] = nt(W[2 * HD : 2 * HD + 4 * count, :], lhs)
-        for copy in swaps(n):
-            copy.start()
+        lhs = T[j : j + GROUP].reshape(GROUP * R, Dh)
+        here = slice(j * R, (j + GROUP) * R)
+        Pn[here, :] = nt(lhs, W[...])
+        PT[:, here] = nt(W[2 * HD : 2 * HD + 4 * count, :], lhs)
+        if j + GROUP == first + slots:
+            for copy in swaps(n):
+                copy.start()
 
     def gather_piece(n):
         first, slots = sets[n]
@@ -312,7 +319,7 @@
         up, down = (slot_of(S, 1, k), slot_of(S, 0, k)) if k <= S // 2 else (slot_of(S, 0, S - k), slot_of(S, 1, S - k))
         return remote(A1.at[up], Att.at[down, rows(x, R), lanes], zS.at[k], zR.at[k], seq=lax.rem(z + k, S))
 
-    far_first = sorted(range(1, S), key=lambda k: -min(k, S - k))
+    outward = sorted(range(1, S), key=lambda k: -min(k, S - k))
 
     def attend():
         lax.fori_loop(0, S, prefix, jnp.zeros((FEATURES, HD), f32))
@@ -324,7 +331,7 @@
                 widened = (num[g, here, :] + far[here, i * HD : (i + 1) * HD]).astype(bf16).astype(f32)
                 power = jnp.mean(widened * widened, axis=1, keepdims=True)
                 A1[GROUP * g + i] = (widened * lax.rsqrt(power + 1e-06) * hgain[...]).astype(bf16)
-        for k in far_first:
+        for k in outward:
             to_plane(k).start()
         Att[0, rows(x, R), lanes] = A1[0]
 
@@ -344,7 +351,7 @@
     share_ring = Ring("fsdp", X, x, share, quarter, quarter // 2, aS, aR)
 
     def arrive(p):
-        for k in far_first:
+        for k in outward:
             down = slot_of(S, 0, k) if k <= S // 2 else slot_of(S, 1, S - k)
             if down // GROUP == p:
                 to_plane(k).wait_recv()
@@ -375,33 +382,37 @@
         jobs.append((time, len(jobs), functools.partial(job, *details)))
 
     half_z, half_x = S // 2, X // 2
+    step_z, step_x, step_o = 5.9, 8.0, 5.2
     for step in range(1, half_z + 1):
-        for p in range(2):
-            at(9.5 + 5.9 * (step - 1) + 2.95 * (p + 1), token_ring.tick, step, p)
+        for p in range(4):
+            at(9.5 + step_z * (step - 1) + step_z / 4 * (p + 1), token_ring.tick, step, p)
     for step in range(1, half_x + 1):
         for p in range(3):
-            at(9.5 + 7.2 * (step - 1) + 2.4 * (p + 1), weight_ring.tick, step, p)
-    held = 9.6 + 7.2 * half_x
-    turn = 9.5 + 5.9 * half_z
+            at(9.5 + step_x * (step - 1) + step_x / 3 * (p + 1), weight_ring.tick, step, p)
+    held = 9.6 + step_x * half_x
+    turn = 9.5 + step_z * half_z
     at(turn - 5.8, out_first)
     at(held, keep_qk)
     free = held
     for n, (first, slots) in enumerate(sets):
-        last = 9.6 + 5.9 * ((first + slots) // 2)
+        last = 9.6 + step_z * ((first + slots) // 2)
         start = max(free, last)
-        at(start, project, n)
-        at(start + 4.0, combine, n)
+        final = n == len(sets) - 1
+        for j in range(first, first + slots, GROUP):
+            at(start + 1.4 * (j - first) / GROUP, project, n, j)
+        joined = start + (3.2 if final else 5.6)
+        at(joined, combine, n)
         if n == 0:
             for step in range(1, half_x + 1):
                 for p in range(2):
-                    at(start + 4.0 + 3.2 * (step - 1) + 1.6 * (p + 1), gather.tick, step, p)
-            end = start + 4.2 + 3.2 * half_x
+                    at(joined + 3.8 * step + 0.8 * p, gather.tick, step, p)
+            end = joined + 3.8 * half_x + 1.0
         else:
-            end = start + 12.5
+            end = joined + (8.8 if final else 11.5)
             at(end, landed, n)
         for g in range(first // GROUP, (first + slots) // GROUP):
             at(end + 0.1, within, g)
-        free = start + 4.1
+        free = start + 1.5 * slots / GROUP
     at(end + 1.0, attend)
     for p in range(quarter):
         at(end + 9.0 + 0.7 * p, arrive, p)
@@ -411,12 +422,12 @@
     for p in range(quarter):
         time = end + 12.0 + 3.2 * half_x + 0.5 * p
         at(time, whole, p)
-        ready = turn + 5.7 * min(2 * p + 2, half_z - 1) + 0.1
+        ready = turn + step_o * min(2 * p + 2, half_z - 1) + 0.1
         at(max(time, ready), product, GROUP * p, min(GROUP * (p + 1), S - 1))
-    at(max(time, turn + 5.7 * half_z) + 0.2, product, S - 1, S)
+    at(max(time, turn + step_o * half_z) + 0.2, product, S - 1, S)
     for step in range(1, half_z + 1):
-        for p in range(2):
-            at(turn + 5.7 * (step - 1) + 2.85 * (p + 1), out_ring.tick, step, p)
+        for p in range(4):
+            at(turn + step_o * (step - 1) + step_o / 4 * (p + 1), out_ring.tick, step, p)
 
     for copy in get_later:
         copy.wait()
@@ -496,10 +507,10 @@
             V((Ppl, C), f32),
             V((2, LANES, 2 * LANES), bf16),
             V((count, 4 * count), bf16),
-            dma((12,)),
-            dma((2, S // 2, 2)), dma((2, S // 2, 2)),
+            dma((14,)),
+            dma((2, S // 2, 4)), dma((2, S // 2, 4)),
             dma((2, X // 2, 3)), dma((2, X // 2, 3)),
-            dma((2, S // 2, 2)), dma((2, S // 2, 2)),
+            dma((2, S // 2, 4)), dma((2, S // 2, 4)),
             dma((2, X // 2, groups)), dma((2, X // 2, groups)),
             dma((2, X // 2, 2)), dma((2, X // 2, 2)),
             dma((len(sets), X, 2)), dma((len(sets), X, 2)),

time: 156 us -> 152 us (0.974)
  Pallas kernels: 152 us -> 150 us
    pallas_call x1, Pallas kernels: 152 us -> 150 us  [per_device(): pl.pallas_call(functools.partial(layer, S, X, sets), out_shape=jax.ShapeD...]
where the time goes in v4:
time: 152 us; the launch traced here: 151 us
  Pallas kernels  150 us (99%)
  local copies, waits for them, and re-layouts  1.67 us (1%)
    pallas_call x1, Pallas kernels, per_device(): pl.pallas_call(functools.partial(layer, S, X, sets), out_shape=jax.ShapeD...  150 us

profile of v4, /device:TPU:65, one launch (start us, length us, event | category | flops | bytes accessed | tf_op | source)
XLA Modules:
  0.0 151.3 jit_solution(2623730184609700868)
XLA Ops:
  0.0 149.6 %layer.1 = bf16[256,512]{1,0:T(8,128)(2,1)} custom-call(bf16[256,8192]{1,0:T(8,128)(2,1)} %tokens.1, f32[1,8192]{1,0:T(1,128)} %bitcast.8, bf16[2,8192]{1,0:T(2,128)(2,1)} %bitcast.9, bf16[2,8192]{1,0:T(2,128)(2,1)} %bitcast.10, bf16[16,8192]{1,0:T(8,128)(2,1)} %bitcast.6, f32[1,128]{1,0:T(1,128)} %bitcast.11, bf16[256,512]{1,0:T(8,128)(2,1)} %bitcast.7, ...), custom_call_target="tpu_custom_call" | custom-call | tf_op jit(solution)/shard_map/layer/pallas_call | solution.py:523
  149.6 1.7 %copy.14 = bf16[256,512]{1,0:T(8,128)(2,1)} copy(bf16[256,512]{1,0:T(8,128)(2,1)} %layer.1) | data formatting | bytes 524288

commit v5 on v4

--- a/solution.py
+++ b/solution.py
@@ -391,7 +391,7 @@
             at(9.5 + step_x * (step - 1) + step_x / 3 * (p + 1), weight_ring.tick, step, p)
     held = 9.6 + step_x * half_x
     turn = 9.5 + step_z * half_z
-    at(turn - 5.8, out_first)
+    at(turn - 8.7, out_first)
     at(held, keep_qk)
     free = held
     for n, (first, slots) in enumerate(sets):
@@ -427,7 +427,7 @@
     at(max(time, turn + step_o * half_z) + 0.2, product, S - 1, S)
     for step in range(1, half_z + 1):
         for p in range(4):
-            at(turn + step_o * (step - 1) + step_o / 4 * (p + 1), out_ring.tick, step, p)
+            at(turn - 2.0 + step_o * (step - 1) + step_o / 4 * (p + 1), out_ring.tick, step, p)
 
     for copy in get_later:
         copy.wait()

time: 152 us -> 152 us (level)
  no operation moved by 1% of the time
where the time goes in v5:
time: 152 us
  Pallas kernels  150 us (99%)
  local copies, waits for them, and re-layouts  1.67 us (1%)
    pallas_call x1, Pallas kernels, per_device(): pl.pallas_call(functools.partial(layer, S, X, sets), out_shape=jax.ShapeD...  150 us

profile of v5, /device:TPU:65, one launch (start us, length us, event | category | flops | bytes accessed | tf_op | source)
XLA Modules:
  0.0 151.8 jit_solution(8397209966214600773)
XLA Ops:
  0.0 150.2 %layer.1 = bf16[256,512]{1,0:T(8,128)(2,1)} custom-call(bf16[256,8192]{1,0:T(8,128)(2,1)} %tokens.1, f32[1,8192]{1,0:T(1,128)} %bitcast.8, bf16[2,8192]{1,0:T(2,128)(2,1)} %bitcast.9, bf16[2,8192]{1,0:T(2,128)(2,1)} %bitcast.10, bf16[16,8192]{1,0:T(8,128)(2,1)} %bitcast.6, f32[1,128]{1,0:T(1,128)} %bitcast.11, bf16[256,512]{1,0:T(8,128)(2,1)} %bitcast.7, ...), custom_call_target="tpu_custom_call" | custom-call | tf_op jit(solution)/shard_map/layer/pallas_call | solution.py:523
  150.2 1.7 %copy.14 = bf16[256,512]{1,0:T(8,128)(2,1)} copy(bf16[256,512]{1,0:T(8,128)(2,1)} %layer.1) | data formatting | bytes 524288
